TPU v7x, 32 devices: a whole 2x2x4 slice. The times are simulated.
32 devices in a mesh: grp: 2 (over x), lat: 16 (over z, y, core).
Axes of the slice: x: 2, y: 2, z: 4, core: 2. Of those that a mesh axis runs over, the one named last changes fastest.
Arguments:
- acts: bfloat16 [128, 2, 2048], P(('grp', 'lat')), parts along dimension 0, may hold values from -6 to 6
- enc_weight: bfloat16 [4, 2048, 4096], P('grp', None, 'lat'), parts along dimension 0, may hold values from -0.09375 to 0.09375
- enc_bias: float32 [8192], P(('grp', 'lat')), parts along dimension 0, may hold values from -3 to 3
- dec_weight: bfloat16 [4096, 4, 2048], P('lat', 'grp'), parts along dimension 1, may hold values from -0.125 to 0.125
- dec_bias: float32 [4, 2048], P('grp'), parts along dimension 0, may hold values from -5 to 5
Outputs:
- residual: bfloat16 [128, 2, 2048], P(('grp', 'lat')), parts along dimension 0
- grad_enc: bfloat16 [4, 2048, 4096], P('grp', None, 'lat'), parts along dimension 0
- grad_enc_bias: float32 [8192], P(('grp', 'lat')), parts along dimension 0
- grad_dec: bfloat16 [4096, 4, 2048], P('lat', 'grp'), parts along dimension 1
- grad_dec_bias: float32 [4, 2048], P('grp'), parts along dimension 0
There are 2 independent parts, one for each index of `grp`. A program takes and returns all parts, laid end to end along the dimension named above; each array names one. Nothing has to cross between parts.
All inputs are finite; a program needn't handle non-finite values.
Results may differ from a plain program's by a relative error of at most 0.015.
Values may be sent and summed in bfloat16 or wider, within the bound.
No kernel may reach another device: no remote copies, remote signals or barrier semaphores. Data moves between devices by JAX's collectives and lax.ppermute only.
A program may use at most 128 MiB of HBM per device.

v0:
```python
import jax
import jax.numpy as jnp
from jax import lax
from jax.sharding import PartitionSpec as P

sparsity_weight = 2.0


def body(acts, enc_weight, enc_bias, dec_weight, dec_bias):
    tok_dev, layers, width = acts.shape
    lat_dev = enc_weight.shape[2]
    wide = layers * width
    total_rows = tok_dev * lax.axis_size("lat")
    factor = 2.0 / total_rows
    flat_rows = acts.reshape(tok_dev, wide)
    flat_enc = enc_weight.reshape(wide, lat_dev)
    flat_dec = dec_weight.reshape(lat_dev, wide)
    flat_bias = dec_bias.reshape(wide)
    own_start = lax.axis_index("lat") * tok_dev
    gathered = lax.all_gather(flat_rows, "lat", axis=0, tiled=True)
    before = jnp.dot(gathered, flat_enc, preferred_element_type=jnp.float32) + enc_bias
    active = jnp.maximum(before, 0.0).astype(jnp.bfloat16)
    dec_wide = dec_weight.astype(jnp.float32)
    row_sq = jnp.sum(dec_wide * dec_wide, axis=2)
    inv_norm = lax.rsqrt(row_sq + 1.0)
    dec_norm = jnp.sum(jnp.sqrt(row_sq + 1.0), axis=1)
    term = jnp.dot(active, flat_dec, preferred_element_type=jnp.float32)
    own_term = lax.dynamic_slice_in_dim(term, own_start, tok_dev, 0)
    own_term = own_term + flat_bias - flat_rows.astype(jnp.float32)
    term = lax.dynamic_update_slice_in_dim(term, own_term, own_start, 0)
    summed = lax.psum(term, "lat")
    all_residual = summed.astype(jnp.bfloat16)
    own_residual = lax.dynamic_slice_in_dim(all_residual, own_start, tok_dev, 0)
    grad_dec_bias = factor * jnp.sum(all_residual.astype(jnp.float32), axis=0)
    dec_total = lax.dot_general(
        active, all_residual, (((0,), (0,)), ((), ())), preferred_element_type=jnp.float32
    )
    backward = lax.dot_general(
        all_residual, flat_dec, (((1,), (1,)), ((), ())), preferred_element_type=jnp.float32
    )
    grad_act = factor * backward + sparsity_weight / total_rows * dec_norm
    grad_before = jnp.where(before > 0.0, grad_act, 0.0).astype(jnp.bfloat16)
    enc_total = lax.dot_general(
        gathered, grad_before, (((0,), (0,)), ((), ())), preferred_element_type=jnp.float32
    )
    grad_enc = enc_total.astype(jnp.bfloat16).reshape(layers, width, lat_dev)
    grad_enc_bias = jnp.sum(grad_before.astype(jnp.float32), axis=0)
    act_sum = jnp.sum(active.astype(jnp.float32), axis=0)
    grad_dec = (
        factor * dec_total.reshape(lat_dev, layers, width)
        + sparsity_weight / total_rows * act_sum[:, None, None] * dec_wide * inv_norm[:, :, None]
    ).astype(jnp.bfloat16)
    return (
        own_residual.reshape(tok_dev, layers, width),
        grad_enc,
        grad_enc_bias,
        grad_dec,
        grad_dec_bias.reshape(layers, width),
    )


def solution(mesh):
    return jax.shard_map(
        body,
        mesh=mesh,
        in_specs=(
            P(("grp", "lat"), None, None),
            P("grp", None, "lat"),
            P(("grp", "lat")),
            P("lat", "grp", None),
            P("grp", None),
        ),
        out_specs=(
            P(("grp", "lat"), None, None),
            P("grp", None, "lat"),
            P(("grp", "lat")),
            P("lat", "grp", None),
            P("grp", None),
        ),
        check_vma=False,
    )
```

profile of v0, /device:TPU:0, one launch (start us, length us, event | category | flops | bytes accessed | tf_op | source)
XLA Modules:
  0.0 136.5 jit_solution(2590079693091624209)
XLA Ops:
  0.6 0.0 copy-start
  0.7 1.6 %copy-done = bf16[2,2048,256]{2,1,0:T(8,128)(2,1)S(1)} copy-done((bf16[2,2048,256]{2,1,0:T(8,128)(2,1)S(1)}, bf16[2,2048,256]{2,1,0:T(8,128)(2,1)}, u32[]{:S(2)}) %copy-start) | copy-done | bytes 2097176
  2.2 0.7 copy.14
  2.9 0.8 reshape.50
  3.7 0.8 convert_bitcast_fusion
  4.5 0.0 copy-start.3
  4.6 3.8 %fusion.1 = f32[256,2]{1,0:T(8,128)S(1)} fusion(bf16[256,2,2048]{2,1,0:T(2,128)(2,1)} %param.8), kind=kLoop, calls=%fused_computation.5 | loop fusion | flops 3145216 | bytes 2099200 | tf_op jit(solution)/shard_map/reduce_sum | solution.py:24
  8.4 0.1 add_rsqrt_fusion
  8.6 24.6 %all-gather = bf16[16,4,4096]{2,1,0:T(4,128)(2,1)S(1)} all-gather(bf16[1,4,4096]{2,1,0:T(4,128)(2,1)S(1)} %reshape.50), channel_id=1, replica_groups=mesh['grp'=2,'lat'=16] {'lat'}, dimensions={0}, use_global_device_ids=true | all-gather | bytes 557056 | tf_op jit(solution)/shard_map/all_gather | solution.py:20
  33.2 0.1 reshape.51
  33.3 0.0 copy-done.3
  33.3 0.0 copy-start.1
  33.3 0.5 convert_reduce_fusion.1
  33.8 1.1 copy-done.1
  34.9 0.9 copy.13
  35.8 0.0 copy-start.2
  35.8 1.3 copy-done.2
  37.1 1.5 %fusion.8 = f32[64,4096]{1,0:T(8,128)} fusion(bf16[256,4096]{1,0:T(8,128)(2,1)S(1)} %bitcast.21, f32[64,256]{1,0:T(8,128)S(1)} %get-tuple-element.20), kind=kOutput, calls=%fused_computation.26 | convolution fusion | flops 134250496 | bytes 3211264 | tf_op jit(solution)/shard_map/dot_general | solution.py:27
  38.6 1.6 %subtract_dynamic-update-slice_fusion = f32[64,4096]{1,0:T(8,128)} fusion(f32[64,4096]{1,0:T(8,128)} %fusion.8, s32[]{:T(128)S(6)} %select_n.9, f32[4,4096]{1,0:T(4,128)S(1)} %bitcast.24, f32[4096]{0:T(1024)S(1)} %bitcast.25), kind=kLoop, calls=%fused_computation.20 | loop fusion | flops 32768 | bytes 212996 | tf_op jit(solution)/shard_map/dynamic_update_slice | solution.py:30
  40.1 70.1 %all-reduce.1 = bf16[64,4096]{1,0:T(8,128)(2,1)S(1)} all-reduce(f32[64,4096]{1,0:T(8,128)} %subtract_dynamic-update-slice_fusion), channel_id=1, replica_groups=mesh['grp'=2,'lat'=16] {'lat'}, use_global_device_ids=true, to_apply=%region_0.0 | all-reduce | flops 262144 | bytes 1572864 | tf_op jit(solution)/shard_map/psum | solution.py:31
  110.2 2.9 %convert_reduce_fusion.2 = (f32[256]{0:T(256)}, bf16[64,256]{1,0:T(8,128)(2,1)S(1)}) fusion(f32[256]{0:T(256)S(1)} %broadcast_multiply_fusion.2, bf16[64,4096]{1,0:T(8,128)(2,1)S(1)} %all-reduce.1, bf16[256,4096]{1,0:T(8,128)(2,1)} %bitcast.22, f32[64,256]{1,0:T(8,128)S(1)} %get-tuple-element.20), kind=kOutput, calls=%fused_computation.19 | convolution fusion | flops 134332160 | bytes 2721792 | tf_op jit(solution)/shard_map/dot_general | solution.py:38
  113.1 0.1 convert_reduce_fusion
  113.3 0.6 mul.82
  113.9 0.7 reshape.48
  114.6 2.0 %fusion = bf16[4096,256]{0,1:T(8,128)(2,1)} fusion(bf16[64,256]{1,0:T(8,128)(2,1)S(1)} %get-tuple-element.18, bf16[64,4096]{1,0:T(8,128)(2,1)S(1)} %reshape.51), kind=kOutput, calls=%fused_computation.4 | convolution fusion | flops 135266304 | bytes 2654208 | tf_op jit(solution)/shard_map/dot_general | solution.py:43
  116.6 4.1 %copy.12 = bf16[4096,256]{1,0:T(8,128)(2,1)} copy(bf16[4096,256]{0,1:T(8,128)(2,1)} %fusion) | data formatting | bytes 4194304
  120.7 2.7 %convolution_multiply_fusion = f32[256,4096]{1,0:T(8,128)} fusion(bf16[64,4096]{1,0:T(8,128)(2,1)S(1)} %all-reduce.1, f32[64,256]{1,0:T(8,128)S(1)} %get-tuple-element.20), kind=kOutput, calls=%fused_computation | convolution fusion | flops 135299072 | bytes 4784128 | tf_op jit(solution)/shard_map/dot_general | solution.py:35
  123.3 6.6 %mul.74 = f32[256,2,2048]{2,1,0:T(2,128)} reshape(f32[256,4096]{1,0:T(8,128)} %convolution_multiply_fusion) | data formatting | bytes 8388608 | tf_op jit(solution)/shard_map/mul | solution.py:50
  129.9 6.7 %fusion.4 = bf16[256,2,2048]{2,1,0:T(2,128)(2,1)} fusion(f32[256,2,2048]{2,1,0:T(2,128)} %mul.74, bf16[256,2,2048]{2,1,0:T(2,128)(2,1)} %param.8, f32[256]{0:T(256)S(1)} %broadcast_multiply_fusion.1, f32[256,2]{1,0:T(8,128)S(1)} %get-tuple-element.15), kind=kLoop, calls=%fused_computation.8 | loop fusion | flops 5242880 | bytes 8391680 | tf_op jit(solution)/shard_map/convert_element_type | solution.py:52
  (5 shorter events, 0.1 us)
Async XLA Ops:
  0.6 1.6 %copy-start = (bf16[2,2048,256]{2,1,0:T(8,128)(2,1)S(1)}, bf16[2,2048,256]{2,1,0:T(8,128)(2,1)}, u32[]{:S(2)}) copy-start(bf16[2,2048,256]{2,1,0:T(8,128)(2,1)} %param.6) | copy-start | bytes 6291460
  4.5 28.8 %copy-start.3 = (f32[256]{0:T(256)S(1)}, f32[256]{0:T(256)}, u32[]{:S(2)}) copy-start(f32[256]{0:T(256)} %param.7) | copy-start | bytes 3076
  33.3 1.6 %copy-start.1 = (bf16[256,2,2048]{2,1,0:T(2,128)(2,1)S(1)}, bf16[256,2,2048]{2,1,0:T(2,128)(2,1)}, u32[]{:S(2)}) copy-start(bf16[256,2,2048]{2,1,0:T(2,128)(2,1)} %param.8) | copy-start | bytes 6291460
  35.8 1.3 copy-start.2
where the time goes:
time: 137 us
  blocking collectives  94.7 us (69%)
  local copies, waits for them, and re-layouts  18.5 us (14%)
  other arithmetic  13.1 us (10%)
  matrix products  9.56 us (7%)
    psum x1, blocking collectives, body(): summed = lax.psum(term, 'lat')  70.1 us
    all_gather x1, blocking collectives, body(): gathered = lax.all_gather(flat_rows, 'lat', axis=0, tiled=True)  24.6 us
    unnamed x14, local copies, waits for them, and re-layouts  10.6 us
    convert_element_type x1, other arithmetic, body(): grad_dec = (factor * dec_total.reshape(lat_dev, layers, width) + sparsity...  6.65 us
    mul x1, local copies, waits for them, and re-layouts, body(): factor * dec_total.reshape(lat_dev, layers, width)  6.57 us
    reduce_sum x1, other arithmetic, body(): row_sq = jnp.sum(dec_wide * dec_wide, axis=2)  3.84 us
    dot_general x1, matrix products, body(): lax.dot_general(all_residual, flat_dec, (((1,), (1,)), ((), ())), preferr...  2.94 us

commit v1 on v0

v1 whole, which is shorter than its diff:
```python
import jax
import jax.numpy as jnp
from jax import lax
from jax.sharding import PartitionSpec as P

sparsity_weight = 2.0


def masks_of(count):
    masks = []
    k = count // 2
    while k:
        masks.append(k)
        k //= 2
    return masks


def swap(x, k, count):
    return lax.ppermute(x, "lat", [(s, s ^ k) for s in range(count)])


def gather_rows(x, count):
    for k in masks_of(count):
        x = jnp.concatenate([x, swap(x, k, count)], axis=0)
    return x


def scatter_rows(term, count):
    for k in reversed(masks_of(count)):
        half = term.shape[0] // 2
        received = swap(term[half:].astype(jnp.bfloat16), k, count)
        term = term[:half] + received.astype(jnp.float32)
    return term


def body(acts, enc_weight, enc_bias, dec_weight, dec_bias):
    tok_dev, layers, width = acts.shape
    lat_dev = enc_weight.shape[2]
    wide = layers * width
    count = lax.axis_size("lat")
    total_rows = tok_dev * count
    factor = 2.0 / total_rows
    flat_rows = acts.reshape(tok_dev, wide)
    flat_enc = enc_weight.reshape(wide, lat_dev)
    flat_dec = lax.optimization_barrier(dec_weight.reshape(lat_dev, wide))
    flat_bias = dec_bias.reshape(wide)
    gathered = gather_rows(flat_rows, count)
    before = jnp.dot(gathered, flat_enc, preferred_element_type=jnp.float32) + enc_bias
    active = jnp.maximum(before, 0.0).astype(jnp.bfloat16)
    term = jnp.dot(active, flat_dec, preferred_element_type=jnp.float32)
    summed = scatter_rows(term, count)
    own_residual = (summed + flat_bias - flat_rows.astype(jnp.float32)).astype(jnp.bfloat16)
    all_residual = gather_rows(own_residual, count)

    layer_dec = [flat_dec[:, l * width : (l + 1) * width].astype(jnp.float32) for l in range(layers)]
    row_sq = [jnp.sum(d * d, axis=1) for d in layer_dec]
    inv_norm = [lax.rsqrt(r + 1.0) for r in row_sq]
    dec_norm = sum(jnp.sqrt(r + 1.0) for r in row_sq)
    gathered_t = lax.optimization_barrier(gathered.T)
    active_t = lax.optimization_barrier(active.T)
    act_sum = jnp.sum(active.astype(jnp.float32), axis=0)

    grad_dec_bias = factor * jnp.sum(all_residual.astype(jnp.float32), axis=0)
    backward = lax.dot_general(
        all_residual, flat_dec, (((1,), (1,)), ((), ())), preferred_element_type=jnp.float32
    )
    grad_act = factor * backward + sparsity_weight / total_rows * dec_norm
    grad_before = jnp.where(before > 0.0, grad_act, 0.0).astype(jnp.bfloat16)
    grad_enc = jnp.dot(gathered_t, grad_before, preferred_element_type=jnp.float32).astype(jnp.bfloat16)
    grad_enc_bias = jnp.sum(grad_before.astype(jnp.float32), axis=0)
    pieces = []
    for l in range(layers):
        total = jnp.dot(
            active_t, all_residual[:, l * width : (l + 1) * width], preferred_element_type=jnp.float32
        )
        scale = sparsity_weight / total_rows * act_sum * inv_norm[l]
        pieces.append((factor * total + scale[:, None] * layer_dec[l]).astype(jnp.bfloat16))
    pieces = lax.optimization_barrier(pieces)
    grad_dec = jnp.stack(pieces, axis=1)
    return (
        own_residual.reshape(tok_dev, layers, width),
        grad_enc.reshape(layers, width, lat_dev),
        grad_enc_bias,
        grad_dec,
        grad_dec_bias.reshape(layers, width),
    )


def solution(mesh):
    return jax.shard_map(
        body,
        mesh=mesh,
        in_specs=(
            P(("grp", "lat"), None, None),
            P("grp", None, "lat"),
            P(("grp", "lat")),
            P("lat", "grp", None),
            P("grp", None),
        ),
        out_specs=(
            P(("grp", "lat"), None, None),
            P("grp", None, "lat"),
            P(("grp", "lat")),
            P("lat", "grp", None),
            P("grp", None),
        ),
        check_vma=False,
    )
```

time: 137 us -> 69.9 us (0.51)
  blocking collectives: 94.7 us -> 0 us
  waiting for transfers between devices: 0 us -> 26.9 us
  starting transfers between devices: 0 us -> 20.5 us
  other arithmetic: 13.1 us -> 1.22 us
  local copies, waits for them, and re-layouts: 18.5 us -> 11.9 us
    psum x1 -> x0, blocking collectives: 70.1 us -> none  [body(): summed = lax.psum(term, 'lat')]
    ppermute x0 -> x12, waiting for transfers between devices: none -> 26.9 us  [swap(): return lax.ppermute(x, 'lat', [(s, s ^ k) for s in range(count)])]
    all_gather x1 -> x0, blocking collectives: 24.6 us -> none  [body(): gathered = lax.all_gather(flat_rows, 'lat', axis=0, tiled=True)]
    ppermute x0 -> x12, starting transfers between devices: none -> 20.5 us  [swap(): return lax.ppermute(x, 'lat', [(s, s ^ k) for s in range(count)])]
    convert_element_type x1 -> x2, other arithmetic: 6.65 us -> 0.04 us  [the longest x1 0.03 us: body(): (summed + flat_bias - flat_rows.astype(jnp.float32)).astype(jnp.bfloat16)]
    mul x1 -> x0, local copies, waits for them, and re-layouts: 6.57 us -> none  [body(): factor * dec_total.reshape(lat_dev, layers, width)]
    reduce_sum x1, other arithmetic: 3.84 us -> 0.48 us  [body(): row_sq = [jnp.sum(d * d, axis=1) for d in layer_dec]]
    dynamic_update_slice x1 -> x0, other arithmetic: 1.56 us -> none  [body(): term = lax.dynamic_update_slice_in_dim(term, own_term, own_start, 0)]
  transfers between devices with their start and end apart: 0 -> 12, of which waited for: 0 -> 11; matrix products, arithmetic and copies ran while one was open for 0% -> 7% of each run, Pallas kernels for 0% -> 0%
where the time goes in v1:
time: 69.9 us; the launch traced here: 69.6 us
  waiting for transfers between devices  26.9 us (38%)
  starting transfers between devices  20.5 us (29%)
  local copies, waits for them, and re-layouts  11.9 us (17%)
  matrix products  8.25 us (12%)
  other arithmetic  1.22 us (2%)
  between operations  0.84 us (1%)
    ppermute x12, waiting for transfers between devices, swap(): return lax.ppermute(x, 'lat', [(s, s ^ k) for s in range(count)])  26.9 us
    ppermute x12, starting transfers between devices, swap(): return lax.ppermute(x, 'lat', [(s, s ^ k) for s in range(count)])  20.5 us
    unnamed x14, local copies, waits for them, and re-layouts  9.39 us
    dot_general x1, matrix products, body(): lax.dot_general(all_residual, flat_dec, (((1,), (1,)), ((), ())), preferr...  2.93 us
    dot_general x2, matrix products, body(): jnp.dot(active_t, all_residual[:, l * width:(l + 1) * width], preferred_e...  2.28 us
    dot_general x1, matrix products, body(): jnp.dot(gathered_t, grad_before, preferred_element_type=jnp.float32)  2.06 us
  transfers between devices with their start and end apart: 12, of which 11 were waited for; matrix products, arithmetic and copies ran while one was open for 7% of the time, Pallas kernels for 0%

profile of v1, /device:TPU:0, one launch (start us, length us, event | category | flops | bytes accessed | tf_op | source)
XLA Modules:
  0.0 69.6 jit_solution(16482156487802836225)
XLA Ops:
  0.6 0.0 copy-start
  0.6 0.9 %copy.11 = bf16[1,4,2,2048]{3,1,2,0:T(4,128)(2,1)S(1)} copy(bf16[1,4,2,2048]{3,2,1,0:T(2,128)(2,1)} %bitcast.40) | data formatting | bytes 65536
  1.6 4.1 %collective-permute-start = (bf16[4,4096]{1,0:T(4,128)(2,1)S(1)}, bf16[4,4096]{1,0:T(4,128)(2,1)S(1)}, u32[]{:S(2)}, u32[]{:S(2)}) collective-permute-start(bf16[4,4096]{1,0:T(4,128)(2,1)S(1)} %bitcast.31), channel_id=1, source_target_pairs={{0,8},{1,9},{2,10},{3,11},{4,12},{5,13},{6,14},{7,15},{8,0},{9,1},... | collective-permute-start | bytes 98312 | tf_op jit(solution)/shard_map/ppermute | solution.py:19
  5.7 2.2 %collective-permute-done = bf16[4,4096]{1,0:T(4,128)(2,1)S(1)} collective-permute-done((bf16[4,4096]{1,0:T(4,128)(2,1)S(1)}, bf16[4,4096]{1,0:T(4,128)(2,1)S(1)}, u32[]{:S(2)}, u32[]{:S(2)}) %collective-permute-start) | collective-permute-done | bytes 32800 | tf_op jit(solution)/shard_map/ppermute | solution.py:19
  8.0 1.6 %collective-permute-start.1 = (bf16[8,4096]{1,0:T(8,128)(2,1)S(1)}, bf16[8,4096]{1,0:T(8,128)(2,1)S(1)}, u32[]{:S(2)}, u32[]{:S(2)}) collective-permute-start(bf16[8,4096]{1,0:T(8,128)(2,1)S(1)} %pad_maximum_fusion.5), channel_id=1, source_target_pairs={{0,4},{1,5},{2,6},{3,7},{4,0},{5,1},{6,2},{7,3},{8,12},{9,13},{10,... | collective-permute-start | bytes 196616 | tf_op jit(solution)/shard_map/ppermute | solution.py:19
  9.6 2.7 %collective-permute-done.1 = bf16[8,4096]{1,0:T(8,128)(2,1)S(1)} collective-permute-done((bf16[8,4096]{1,0:T(8,128)(2,1)S(1)}, bf16[8,4096]{1,0:T(8,128)(2,1)S(1)}, u32[]{:S(2)}, u32[]{:S(2)}) %collective-permute-start.1) | collective-permute-done | bytes 65568 | tf_op jit(solution)/shard_map/ppermute | solution.py:19
  12.3 0.1 pad_maximum_fusion.3
  12.4 1.8 %collective-permute-start.2 = (bf16[16,4096]{1,0:T(8,128)(2,1)S(1)}, bf16[16,4096]{1,0:T(8,128)(2,1)S(1)}, u32[]{:S(2)}, u32[]{:S(2)}) collective-permute-start(bf16[16,4096]{1,0:T(8,128)(2,1)S(1)} %pad_maximum_fusion.3), channel_id=1, source_target_pairs={{0,2},{1,3},{2,0},{3,1},{4,6},{5,7},{6,4},{7,5},{8,10},{9,11},{10,... | collective-permute-start | bytes 393224 | tf_op jit(solution)/shard_map/ppermute | solution.py:19
  14.2 3.2 %collective-permute-done.2 = bf16[16,4096]{1,0:T(8,128)(2,1)S(1)} collective-permute-done((bf16[16,4096]{1,0:T(8,128)(2,1)S(1)}, bf16[16,4096]{1,0:T(8,128)(2,1)S(1)}, u32[]{:S(2)}, u32[]{:S(2)}) %collective-permute-start.2) | collective-permute-done | bytes 131104 | tf_op jit(solution)/shard_map/ppermute | solution.py:19
  17.4 0.1 pad_maximum_fusion.1
  17.5 0.1 collective-permute-start.3
  17.6 0.0 copy-start.4
  17.6 3.8 %copy.12 = bf16[32,8,2,2048]{3,1,2,0:T(8,128)(2,1)} copy(bf16[32,8,2,2048]{3,2,1,0:T(2,128)(2,1)} %bitcast.29) | data formatting | bytes 4194304
  21.4 0.0 collective-permute-done.3
  21.4 0.2 concatenate.33
  21.5 0.0 copy-done
  21.5 0.0 copy-start.1
  21.6 0.0 copy-done.4
  21.6 0.5 convert_reduce_fusion.1
  22.1 1.1 %copy-done.1 = bf16[32,8,2,2048]{3,1,2,0:T(8,128)(2,1)S(1)} copy-done((bf16[32,8,2,2048]{3,1,2,0:T(8,128)(2,1)S(1)}, bf16[32,8,2,2048]{3,1,2,0:T(8,128)(2,1)}, u32[]{:S(2)}) %copy-start.1) | copy-done | bytes 2097176
  23.1 0.5 fusion.13
  23.6 0.0 copy-start.3
  23.7 0.6 collective-permute-start.4
  24.2 1.2 %collective-permute-done.4 = bf16[32,4096]{1,0:T(8,128)(2,1)S(1)} collective-permute-done((bf16[32,4096]{1,0:T(8,128)(2,1)S(1)}, bf16[32,4096]{1,0:T(8,128)(2,1)S(1)}, u32[]{:S(2)}, u32[]{:S(2)}) %collective-permute-start.4) | collective-permute-done | bytes 262176 | tf_op jit(solution)/shard_map/ppermute | solution.py:19
  25.5 1.8 %collective-permute-start.5 = (bf16[16,4096]{1,0:T(8,128)(2,1)S(1)}, bf16[16,4096]{1,0:T(8,128)(2,1)S(1)}, u32[]{:S(2)}, u32[]{:S(2)}) collective-permute-start(bf16[16,4096]{1,0:T(8,128)(2,1)S(1)} %slice.87), channel_id=1, source_target_pairs={{0,2},{1,3},{2,0},{3,1},{4,6},{5,7},{6,4},{7,5},{8,10},{9,11},{10,... | collective-permute-start | bytes 393224 | tf_op jit(solution)/shard_map/ppermute | solution.py:19
  27.3 4.0 %collective-permute-done.5 = bf16[16,4096]{1,0:T(8,128)(2,1)S(1)} collective-permute-done((bf16[16,4096]{1,0:T(8,128)(2,1)S(1)}, bf16[16,4096]{1,0:T(8,128)(2,1)S(1)}, u32[]{:S(2)}, u32[]{:S(2)}) %collective-permute-start.5) | collective-permute-done | bytes 131104 | tf_op jit(solution)/shard_map/ppermute | solution.py:19
  31.4 1.6 %collective-permute-start.6 = (bf16[8,4096]{1,0:T(8,128)(2,1)S(1)}, bf16[8,4096]{1,0:T(8,128)(2,1)S(1)}, u32[]{:S(2)}, u32[]{:S(2)}) collective-permute-start(bf16[8,4096]{1,0:T(8,128)(2,1)S(1)} %slice.88), channel_id=1, source_target_pairs={{0,4},{1,5},{2,6},{3,7},{4,0},{5,1},{6,2},{7,3},{8,12},{9,13},{10,... | collective-permute-start | bytes 196616 | tf_op jit(solution)/shard_map/ppermute | solution.py:19
  33.0 2.7 %collective-permute-done.6 = bf16[8,4096]{1,0:T(8,128)(2,1)S(1)} collective-permute-done((bf16[8,4096]{1,0:T(8,128)(2,1)S(1)}, bf16[8,4096]{1,0:T(8,128)(2,1)S(1)}, u32[]{:S(2)}, u32[]{:S(2)}) %collective-permute-start.6) | collective-permute-done | bytes 65568 | tf_op jit(solution)/shard_map/ppermute | solution.py:19
  35.7 2.7 %collective-permute-start.7 = (bf16[4,4096]{1,0:T(4,128)(2,1)S(1)}, bf16[4,4096]{1,0:T(4,128)(2,1)S(1)}, u32[]{:S(2)}, u32[]{:S(2)}) collective-permute-start(bf16[4,4096]{1,0:T(4,128)(2,1)S(1)} %slice.89), channel_id=1, source_target_pairs={{0,8},{1,9},{2,10},{3,11},{4,12},{5,13},{6,14},{7,15},{8,0},{9,1},... | collective-permute-start | bytes 98312 | tf_op jit(solution)/shard_map/ppermute | solution.py:19
  38.4 0.0 copy-done.3
  38.4 2.2 %collective-permute-done.7 = bf16[4,4096]{1,0:T(4,128)(2,1)S(1)} collective-permute-done((bf16[4,4096]{1,0:T(4,128)(2,1)S(1)}, bf16[4,4096]{1,0:T(4,128)(2,1)S(1)}, u32[]{:S(2)}, u32[]{:S(2)}) %collective-permute-start.7) | collective-permute-done | bytes 32800 | tf_op jit(solution)/shard_map/ppermute | solution.py:19
  40.6 2.7 %collective-permute-start.8 = (bf16[4,4096]{1,0:T(4,128)(2,1)S(1)}, bf16[4,4096]{1,0:T(4,128)(2,1)S(1)}, u32[]{:S(2)}, u32[]{:S(2)}) collective-permute-start(bf16[4,4096]{1,0:T(4,128)(2,1)S(1)} %fusion.11), channel_id=1, source_target_pairs={{0,8},{1,9},{2,10},{3,11},{4,12},{5,13},{6,14},{7,15},{8,0},{9,1},... | collective-permute-start | bytes 98312 | tf_op jit(solution)/shard_map/ppermute | solution.py:19
  43.3 2.2 %collective-permute-done.8 = bf16[4,4096]{1,0:T(4,128)(2,1)S(1)} collective-permute-done((bf16[4,4096]{1,0:T(4,128)(2,1)S(1)}, bf16[4,4096]{1,0:T(4,128)(2,1)S(1)}, u32[]{:S(2)}, u32[]{:S(2)}) %collective-permute-start.8) | collective-permute-done | bytes 32800 | tf_op jit(solution)/shard_map/ppermute | solution.py:19
  45.6 1.7 %collective-permute-start.9 = (bf16[8,4096]{1,0:T(8,128)(2,1)S(1)}, bf16[8,4096]{1,0:T(8,128)(2,1)S(1)}, u32[]{:S(2)}, u32[]{:S(2)}) collective-permute-start(bf16[8,4096]{1,0:T(8,128)(2,1)S(1)} %pad_maximum_fusion.6), channel_id=1, source_target_pairs={{0,4},{1,5},{2,6},{3,7},{4,0},{5,1},{6,2},{7,3},{8,12},{9,13},{10,... | collective-permute-start | bytes 196616 | tf_op jit(solution)/shard_map/ppermute | solution.py:19
  47.3 2.6 %collective-permute-done.9 = bf16[8,4096]{1,0:T(8,128)(2,1)S(1)} collective-permute-done((bf16[8,4096]{1,0:T(8,128)(2,1)S(1)}, bf16[8,4096]{1,0:T(8,128)(2,1)S(1)}, u32[]{:S(2)}, u32[]{:S(2)}) %collective-permute-start.9) | collective-permute-done | bytes 65568 | tf_op jit(solution)/shard_map/ppermute | solution.py:19
  49.9 0.1 pad_maximum_fusion.4
  50.0 1.8 %collective-permute-start.10 = (bf16[16,4096]{1,0:T(8,128)(2,1)S(1)}, bf16[16,4096]{1,0:T(8,128)(2,1)S(1)}, u32[]{:S(2)}, u32[]{:S(2)}) collective-permute-start(bf16[16,4096]{1,0:T(8,128)(2,1)S(1)} %pad_maximum_fusion.4), channel_id=1, source_target_pairs={{0,2},{1,3},{2,0},{3,1},{4,6},{5,7},{6,4},{7,5},{8,10},{9,11},{10,... | collective-permute-start | bytes 393224 | tf_op jit(solution)/shard_map/ppermute | solution.py:19
  51.8 0.5 fusion.4
  52.2 2.8 %collective-permute-done.10 = bf16[16,4096]{1,0:T(8,128)(2,1)S(1)} collective-permute-done((bf16[16,4096]{1,0:T(8,128)(2,1)S(1)}, bf16[16,4096]{1,0:T(8,128)(2,1)S(1)}, u32[]{:S(2)}, u32[]{:S(2)}) %collective-permute-start.10) | collective-permute-done | bytes 131104 | tf_op jit(solution)/shard_map/ppermute | solution.py:19
  55.0 0.1 pad_maximum_fusion.2
  55.1 0.1 collective-permute-start.11
  55.2 0.7 reshape.59
  55.8 1.0 %collective-permute-done.11 = bf16[32,4096]{1,0:T(8,128)(2,1)} collective-permute-done((bf16[32,4096]{1,0:T(8,128)(2,1)S(1)}, bf16[32,4096]{1,0:T(8,128)(2,1)}, u32[]{:S(2)}, u32[]{:S(2)}) %collective-permute-start.11) | collective-permute-done | bytes 262176 | tf_op jit(solution)/shard_map/ppermute | solution.py:19
  56.8 1.1 %concatenate.37 = bf16[64,4096]{1,0:T(8,128)(2,1)S(1)} concatenate(bf16[4,4096]{1,0:T(4,128)(2,1)S(1)} %fusion.11, bf16[4,4096]{1,0:T(4,128)(2,1)S(1)} %collective-permute-done.8, bf16[8,4096]{1,0:T(8,128)(2,1)S(1)} %collective-permute-done.9, bf16[16,4096]{1,0:T(8,128)(2,1)S(1)} %collective-permute-done.10, bf16[32,4096]{1,0:T(8,128)(2,1)} %collective-permute-done.11), dimensions={0} | concatenate | bytes 1048576 | tf_op jit(solution)/shard_map/concatenate | solution.py:24
  57.9 0.1 convert_reduce_fusion
  58.0 2.9 %convert_reduce_fusion.2 = (f32[256]{0:T(256)}, bf16[64,256]{1,0:T(8,128)(2,1)S(1)}) fusion(f32[256]{0:T(256)S(1)} %get-tuple-element.17, bf16[64,4096]{1,0:T(8,128)(2,1)S(1)} %concatenate.37, bf16[256,4096]{1,0:T(8,128)(2,1)} %bitcast.23, f32[64,256]{1,0:T(8,128)S(1)} %get-tuple-element.20), kind=kOutput, calls=%fused_computation.38 | convolution fusion | flops 134332160 | bytes 2721792 | tf_op jit(solution)/shard_map/dot_general | solution.py:64
  60.9 0.6 mul.92
  61.5 0.0 copy-start.2
  61.5 1.8 %fusion.3 = bf16[256,2048]{1,0:T(8,128)(2,1)S(1)} fusion(bf16[256,64]{0,1:T(8,128)(2,1)S(1)} %fusion.12, f32[256]{0:T(256)S(1)} %get-tuple-element.16, bf16[256,4096]{1,0:T(8,128)(2,1)} %bitcast.24, bf16[64,4096]{1,0:T(8,128)(2,1)S(1)} %concatenate.37), kind=kOutput, calls=%fused_computation.10 | convolution fusion | flops 69730304 | bytes 2393088 | tf_op jit(solution)/shard_map/dot_general | solution.py:73
  63.4 0.1 copy-done.2
  63.4 0.5 fusion.2
  63.9 0.2 pad_maximum_fusion
  64.1 3.5 %copy.10 = bf16[256,2,2048]{2,1,0:T(2,128)(2,1)} copy(bf16[256,2,2048]{2,0,1:T(8,128)(2,1)S(1)} %pad_maximum_fusion) | data formatting | bytes 4194304
  67.6 2.1 %convolution_convert_fusion = bf16[4096,256]{1,0:T(8,128)(2,1)} fusion(bf16[4096,64]{0,1:T(8,128)(2,1)S(1)} %bitcast.28, bf16[64,256]{1,0:T(8,128)(2,1)S(1)} %get-tuple-element.22), kind=kOutput, calls=%fused_computation | convolution fusion | flops 135266304 | bytes 2654208 | tf_op jit(solution)/shard_map/dot_general | solution.py:69
  (14 shorter events, 0.3 us)
Async XLA Ops:
  0.6 20.9 %copy-start = (bf16[2,2048,256]{2,1,0:T(8,128)(2,1)S(1)}, bf16[2,2048,256]{2,1,0:T(8,128)(2,1)}, u32[]{:S(2)}) copy-start(bf16[2,2048,256]{2,1,0:T(8,128)(2,1)} %param.6) | copy-start | bytes 6291460
  1.6 6.4 %collective-permute-start = (bf16[4,4096]{1,0:T(4,128)(2,1)S(1)}, bf16[4,4096]{1,0:T(4,128)(2,1)S(1)}, u32[]{:S(2)}, u32[]{:S(2)}) collective-permute-start(bf16[4,4096]{1,0:T(4,128)(2,1)S(1)} %bitcast.31), channel_id=1, source_target_pairs={{0,8},{1,9},{2,10},{3,11},{4,12},{5,13},{6,14},{7,15},{8,0},{9,1},... | collective-permute-start | bytes 98312 | tf_op jit(solution)/shard_map/ppermute | solution.py:19
  8.0 4.3 %collective-permute-start.1 = (bf16[8,4096]{1,0:T(8,128)(2,1)S(1)}, bf16[8,4096]{1,0:T(8,128)(2,1)S(1)}, u32[]{:S(2)}, u32[]{:S(2)}) collective-permute-start(bf16[8,4096]{1,0:T(8,128)(2,1)S(1)} %pad_maximum_fusion.5), channel_id=1, source_target_pairs={{0,4},{1,5},{2,6},{3,7},{4,0},{5,1},{6,2},{7,3},{8,12},{9,13},{10,... | collective-permute-start | bytes 196616 | tf_op jit(solution)/shard_map/ppermute | solution.py:19
  12.4 5.0 %collective-permute-start.2 = (bf16[16,4096]{1,0:T(8,128)(2,1)S(1)}, bf16[16,4096]{1,0:T(8,128)(2,1)S(1)}, u32[]{:S(2)}, u32[]{:S(2)}) collective-permute-start(bf16[16,4096]{1,0:T(8,128)(2,1)S(1)} %pad_maximum_fusion.3), channel_id=1, source_target_pairs={{0,2},{1,3},{2,0},{3,1},{4,6},{5,7},{6,4},{7,5},{8,10},{9,11},{10,... | collective-permute-start | bytes 393224 | tf_op jit(solution)/shard_map/ppermute | solution.py:19
  17.5 3.9 %collective-permute-start.3 = (bf16[32,4096]{1,0:T(8,128)(2,1)S(1)}, bf16[32,4096]{1,0:T(8,128)(2,1)S(1)}, u32[]{:S(2)}, u32[]{:S(2)}) collective-permute-start(bf16[32,4096]{1,0:T(8,128)(2,1)S(1)} %pad_maximum_fusion.1), channel_id=1, source_target_pairs={{0,1},{1,0},{2,3},{3,2},{4,5},{5,4},{6,7},{7,6},{8,9},{9,8},{10,11... | collective-permute-start | bytes 786440 | tf_op jit(solution)/shard_map/ppermute | solution.py:19
  17.6 4.0 %copy-start.4 = (f32[256]{0:T(256)S(1)}, f32[256]{0:T(256)}, u32[]{:S(2)}) copy-start(f32[256]{0:T(256)} %param.7) | copy-start | bytes 3076
  21.5 1.6 %copy-start.1 = (bf16[32,8,2,2048]{3,1,2,0:T(8,128)(2,1)S(1)}, bf16[32,8,2,2048]{3,1,2,0:T(8,128)(2,1)}, u32[]{:S(2)}) copy-start(bf16[32,8,2,2048]{3,1,2,0:T(8,128)(2,1)} %copy.12) | copy-start | bytes 6291460
  23.6 14.8 %copy-start.3 = (f32[2,2048]{1,0:T(2,128)S(1)}, f32[2,2048]{1,0:T(2,128)}, u32[]{:S(2)}) copy-start(f32[2,2048]{1,0:T(2,128)} %param.9) | copy-start | bytes 49156
  23.7 1.7 %collective-permute-start.4 = (bf16[32,4096]{1,0:T(8,128)(2,1)S(1)}, bf16[32,4096]{1,0:T(8,128)(2,1)S(1)}, u32[]{:S(2)}, u32[]{:S(2)}) collective-permute-start(bf16[32,4096]{1,0:T(8,128)(2,1)S(1)} %slice.86), channel_id=1, source_target_pairs={{0,1},{1,0},{2,3},{3,2},{4,5},{5,4},{6,7},{7,6},{8,9},{9,8},{10,11... | collective-permute-start | bytes 786440 | tf_op jit(solution)/shard_map/ppermute | solution.py:19
  25.5 5.8 %collective-permute-start.5 = (bf16[16,4096]{1,0:T(8,128)(2,1)S(1)}, bf16[16,4096]{1,0:T(8,128)(2,1)S(1)}, u32[]{:S(2)}, u32[]{:S(2)}) collective-permute-start(bf16[16,4096]{1,0:T(8,128)(2,1)S(1)} %slice.87), channel_id=1, source_target_pairs={{0,2},{1,3},{2,0},{3,1},{4,6},{5,7},{6,4},{7,5},{8,10},{9,11},{10,... | collective-permute-start | bytes 393224 | tf_op jit(solution)/shard_map/ppermute | solution.py:19
  31.4 4.3 %collective-permute-start.6 = (bf16[8,4096]{1,0:T(8,128)(2,1)S(1)}, bf16[8,4096]{1,0:T(8,128)(2,1)S(1)}, u32[]{:S(2)}, u32[]{:S(2)}) collective-permute-start(bf16[8,4096]{1,0:T(8,128)(2,1)S(1)} %slice.88), channel_id=1, source_target_pairs={{0,4},{1,5},{2,6},{3,7},{4,0},{5,1},{6,2},{7,3},{8,12},{9,13},{10,... | collective-permute-start | bytes 196616 | tf_op jit(solution)/shard_map/ppermute | solution.py:19
  35.7 4.9 %collective-permute-start.7 = (bf16[4,4096]{1,0:T(4,128)(2,1)S(1)}, bf16[4,4096]{1,0:T(4,128)(2,1)S(1)}, u32[]{:S(2)}, u32[]{:S(2)}) collective-permute-start(bf16[4,4096]{1,0:T(4,128)(2,1)S(1)} %slice.89), channel_id=1, source_target_pairs={{0,8},{1,9},{2,10},{3,11},{4,12},{5,13},{6,14},{7,15},{8,0},{9,1},... | collective-permute-start | bytes 98312 | tf_op jit(solution)/shard_map/ppermute | solution.py:19
  40.6 4.9 %collective-permute-start.8 = (bf16[4,4096]{1,0:T(4,128)(2,1)S(1)}, bf16[4,4096]{1,0:T(4,128)(2,1)S(1)}, u32[]{:S(2)}, u32[]{:S(2)}) collective-permute-start(bf16[4,4096]{1,0:T(4,128)(2,1)S(1)} %fusion.11), channel_id=1, source_target_pairs={{0,8},{1,9},{2,10},{3,11},{4,12},{5,13},{6,14},{7,15},{8,0},{9,1},... | collective-permute-start | bytes 98312 | tf_op jit(solution)/shard_map/ppermute | solution.py:19
  45.6 4.3 %collective-permute-start.9 = (bf16[8,4096]{1,0:T(8,128)(2,1)S(1)}, bf16[8,4096]{1,0:T(8,128)(2,1)S(1)}, u32[]{:S(2)}, u32[]{:S(2)}) collective-permute-start(bf16[8,4096]{1,0:T(8,128)(2,1)S(1)} %pad_maximum_fusion.6), channel_id=1, source_target_pairs={{0,4},{1,5},{2,6},{3,7},{4,0},{5,1},{6,2},{7,3},{8,12},{9,13},{10,... | collective-permute-start | bytes 196616 | tf_op jit(solution)/shard_map/ppermute | solution.py:19
  50.0 5.0 %collective-permute-start.10 = (bf16[16,4096]{1,0:T(8,128)(2,1)S(1)}, bf16[16,4096]{1,0:T(8,128)(2,1)S(1)}, u32[]{:S(2)}, u32[]{:S(2)}) collective-permute-start(bf16[16,4096]{1,0:T(8,128)(2,1)S(1)} %pad_maximum_fusion.4), channel_id=1, source_target_pairs={{0,2},{1,3},{2,0},{3,1},{4,6},{5,7},{6,4},{7,5},{8,10},{9,11},{10,... | collective-permute-start | bytes 393224 | tf_op jit(solution)/shard_map/ppermute | solution.py:19
  55.1 1.7 %collective-permute-start.11 = (bf16[32,4096]{1,0:T(8,128)(2,1)S(1)}, bf16[32,4096]{1,0:T(8,128)(2,1)}, u32[]{:S(2)}, u32[]{:S(2)}) collective-permute-start(bf16[32,4096]{1,0:T(8,128)(2,1)S(1)} %pad_maximum_fusion.2), channel_id=1, source_target_pairs={{0,1},{1,0},{2,3},{3,2},{4,5},{5,4},{6,7},{7,6},{8,9},{9,8},{10,11... | collective-permute-start | bytes 786440 | tf_op jit(solution)/shard_map/ppermute | solution.py:19
  61.5 1.9 %copy-start.2 = (bf16[32,8,2,2048]{3,1,2,0:T(8,128)(2,1)S(1)}, bf16[32,8,2,2048]{3,1,2,0:T(8,128)(2,1)}, u32[]{:S(2)}) copy-start(bf16[32,8,2,2048]{3,1,2,0:T(8,128)(2,1)} %copy.12) | copy-start | bytes 6291460

commit v2 on v1

--- a/solution.py
+++ b/solution.py
@@ -19,17 +19,33 @@
     return lax.ppermute(x, "lat", [(s, s ^ k) for s in range(count)])
 
 
-def gather_rows(x, count):
-    for k in masks_of(count):
+def gather_rows(x, count, direct, side=None):
+    masks = masks_of(count)
+    if direct and len(masks) > 2:
+        far, near = masks[:2]
+        parts = [x] + [swap(x, k, count) for k in (far, near, far ^ near)]
+        x = jnp.concatenate(parts, axis=0)
+        masks = masks[2:]
+    for k in masks:
+        if side is not None and k == 1:
+            x, side = lax.optimization_barrier((x, side))
         x = jnp.concatenate([x, swap(x, k, count)], axis=0)
-    return x
+    return x if side is None else (x, side)
 
 
-def scatter_rows(term, count):
-    for k in reversed(masks_of(count)):
+def scatter_rows(term, count, direct):
+    masks = masks_of(count)
+    last = masks[:2] if direct and len(masks) > 2 else []
+    for k in reversed(masks[len(last) :]):
         half = term.shape[0] // 2
         received = swap(term[half:].astype(jnp.bfloat16), k, count)
         term = term[:half] + received.astype(jnp.float32)
+    if last:
+        far, near = last
+        rows = term.shape[0] // 4
+        blocks = [term[p * rows : (p + 1) * rows] for p in range(4)]
+        got = [swap(b.astype(jnp.bfloat16), k, count) for b, k in zip(blocks[1:], (far, near, far ^ near))]
+        term = blocks[0] + sum(g.astype(jnp.float32) for g in got)
     return term
 
 
@@ -44,13 +60,13 @@
     flat_enc = enc_weight.reshape(wide, lat_dev)
     flat_dec = lax.optimization_barrier(dec_weight.reshape(lat_dev, wide))
     flat_bias = dec_bias.reshape(wide)
-    gathered = gather_rows(flat_rows, count)
+    gathered, flat_dec = gather_rows(flat_rows, count, True, flat_dec)
     before = jnp.dot(gathered, flat_enc, preferred_element_type=jnp.float32) + enc_bias
     active = jnp.maximum(before, 0.0).astype(jnp.bfloat16)
     term = jnp.dot(active, flat_dec, preferred_element_type=jnp.float32)
-    summed = scatter_rows(term, count)
+    summed = scatter_rows(term, count, True)
     own_residual = (summed + flat_bias - flat_rows.astype(jnp.float32)).astype(jnp.bfloat16)
-    all_residual = gather_rows(own_residual, count)
+    all_residual = gather_rows(own_residual, count, True)
 
     layer_dec = [flat_dec[:, l * width : (l + 1) * width].astype(jnp.float32) for l in range(layers)]
     row_sq = [jnp.sum(d * d, axis=1) for d in layer_dec]

time: 69.9 us -> 62.4 us (0.89)
  waiting for transfers between devices: 26.9 us -> 22 us
  starting transfers between devices: 20.5 us -> 18.9 us
  local copies, waits for them, and re-layouts: 11.9 us -> 11 us
    ppermute x12 -> x15, waiting for transfers between devices: 26.9 us -> 22 us  [swap(): return lax.ppermute(x, 'lat', [(s, s ^ k) for s in range(count)])]
    ppermute x12 -> x15, starting transfers between devices: 20.5 us -> 18.9 us  [swap(): return lax.ppermute(x, 'lat', [(s, s ^ k) for s in range(count)])]
    unnamed x14 -> x15, local copies, waits for them, and re-layouts: 9.39 us -> 8.33 us
  transfers between devices with their start and end apart: 12 -> 15, of which waited for: 11 -> 14; matrix products, arithmetic and copies ran while one was open for 7% -> 8% of each run, Pallas kernels for 0% -> 0%
where the time goes in v2:
time: 62.4 us; the launch traced here: 62.1 us
  waiting for transfers between devices  22 us (35%)
  starting transfers between devices  18.9 us (30%)
  local copies, waits for them, and re-layouts  11 us (18%)
  matrix products  8.23 us (13%)
  other arithmetic  1.1 us (2%)
  between operations  0.84 us (1%)
    ppermute x15, waiting for transfers between devices, swap(): return lax.ppermute(x, 'lat', [(s, s ^ k) for s in range(count)])  22 us
    ppermute x15, starting transfers between devices, swap(): return lax.ppermute(x, 'lat', [(s, s ^ k) for s in range(count)])  18.9 us
    unnamed x15, local copies, waits for them, and re-layouts  8.33 us
    dot_general x1, matrix products, body(): lax.dot_general(all_residual, flat_dec, (((1,), (1,)), ((), ())), preferr...  2.93 us
    dot_general x2, matrix products, body(): jnp.dot(active_t, all_residual[:, l * width:(l + 1) * width], preferred_e...  2.28 us
    dot_general x1, matrix products, body(): jnp.dot(gathered_t, grad_before, preferred_element_type=jnp.float32)  2.06 us
    concatenate x4, local copies, waits for them, and re-layouts, gather_rows(): x = jnp.concatenate([x, swap(x, k, count)], axis=0)  1.33 us
  transfers between devices with their start and end apart: 15, of which 14 were waited for; matrix products, arithmetic and copies ran while one was open for 8% of the time, Pallas kernels for 0%

profile of v2, /device:TPU:0, one launch (start us, length us, event | category | flops | bytes accessed | tf_op | source)
XLA Modules:
  0.0 62.1 jit_solution(12654589810557397322)
XLA Ops:
  0.6 0.0 copy-start
  0.6 0.9 %copy.11 = bf16[1,4,2,2048]{3,1,2,0:T(4,128)(2,1)S(1)} copy(bf16[1,4,2,2048]{3,2,1,0:T(2,128)(2,1)} %bitcast.40) | data formatting | bytes 65536
  1.6 5.1 %collective-permute-start.2 = (bf16[4,4096]{1,0:T(4,128)(2,1)S(1)}, bf16[4,4096]{1,0:T(4,128)(2,1)S(1)}, u32[]{:S(2)}, u32[]{:S(2)}) collective-permute-start(bf16[4,4096]{1,0:T(4,128)(2,1)S(1)} %bitcast.33), channel_id=1, source_target_pairs={{0,12},{1,13},{2,14},{3,15},{4,8},{5,9},{6,10},{7,11},{8,4},{9,5},... | collective-permute-start | bytes 98312 | tf_op jit(solution)/shard_map/ppermute | solution.py:19
  6.7 0.0 collective-permute-start.1
  6.7 0.6 %collective-permute-start = (bf16[4,4096]{1,0:T(4,128)(2,1)S(1)}, bf16[4,4096]{1,0:T(4,128)(2,1)S(1)}, u32[]{:S(2)}, u32[]{:S(2)}) collective-permute-start(bf16[4,4096]{1,0:T(4,128)(2,1)S(1)} %bitcast.35), channel_id=1, source_target_pairs={{0,8},{1,9},{2,10},{3,11},{4,12},{5,13},{6,14},{7,15},{8,0},{9,1},... | collective-permute-start | bytes 98312 | tf_op jit(solution)/shard_map/ppermute | solution.py:19
  7.4 1.3 %collective-permute-done.2 = bf16[4,4096]{1,0:T(4,128)(2,1)S(1)} collective-permute-done((bf16[4,4096]{1,0:T(4,128)(2,1)S(1)}, bf16[4,4096]{1,0:T(4,128)(2,1)S(1)}, u32[]{:S(2)}, u32[]{:S(2)}) %collective-permute-start.2) | collective-permute-done | bytes 32800 | tf_op jit(solution)/shard_map/ppermute | solution.py:19
  8.6 2.0 %collective-permute-done.1 = bf16[4,4096]{1,0:T(4,128)(2,1)S(1)} collective-permute-done((bf16[4,4096]{1,0:T(4,128)(2,1)S(1)}, bf16[4,4096]{1,0:T(4,128)(2,1)S(1)}, u32[]{:S(2)}, u32[]{:S(2)}) %collective-permute-start.1) | collective-permute-done | bytes 32800 | tf_op jit(solution)/shard_map/ppermute | solution.py:19
  10.6 1.0 %collective-permute-done = bf16[4,4096]{1,0:T(4,128)(2,1)S(1)} collective-permute-done((bf16[4,4096]{1,0:T(4,128)(2,1)S(1)}, bf16[4,4096]{1,0:T(4,128)(2,1)S(1)}, u32[]{:S(2)}, u32[]{:S(2)}) %collective-permute-start) | collective-permute-done | bytes 32800 | tf_op jit(solution)/shard_map/ppermute | solution.py:19
  11.6 0.1 pad_maximum_fusion.1
  11.7 1.6 %collective-permute-start.3 = (bf16[16,4096]{1,0:T(8,128)(2,1)S(1)}, bf16[16,4096]{1,0:T(8,128)(2,1)S(1)}, u32[]{:S(2)}, u32[]{:S(2)}) collective-permute-start(bf16[16,4096]{1,0:T(8,128)(2,1)S(1)} %pad_maximum_fusion.1), channel_id=1, source_target_pairs={{0,2},{1,3},{2,0},{3,1},{4,6},{5,7},{6,4},{7,5},{8,10},{9,11},{10,... | collective-permute-start | bytes 393224 | tf_op jit(solution)/shard_map/ppermute | solution.py:19
  13.3 0.0 copy-start.4
  13.3 3.8 %copy.12 = bf16[32,8,2,2048]{3,1,2,0:T(8,128)(2,1)} copy(bf16[32,8,2,2048]{3,2,1,0:T(2,128)(2,1)} %bitcast.29) | data formatting | bytes 4194304
  17.1 0.0 collective-permute-done.3
  17.1 0.1 concatenate.22
  17.2 0.0 copy-start.1
  17.3 0.1 collective-permute-start.4
  17.4 1.5 %collective-permute-done.4 = bf16[32,4096]{1,0:T(8,128)(2,1)S(1)} collective-permute-done((bf16[32,4096]{1,0:T(8,128)(2,1)S(1)}, bf16[32,4096]{1,0:T(8,128)(2,1)S(1)}, u32[]{:S(2)}, u32[]{:S(2)}) %collective-permute-start.4) | collective-permute-done | bytes 262176 | tf_op jit(solution)/shard_map/ppermute | solution.py:19
  18.9 0.0 copy-done
  18.9 0.0 copy-done.4
  18.9 0.5 convert_reduce_fusion.1
  19.4 0.0 copy-done.1
  19.4 0.5 fusion.13
  19.9 0.0 copy-start.3
  19.9 0.2 collective-permute-start.5
  20.1 1.4 %collective-permute-done.5 = bf16[32,4096]{1,0:T(8,128)(2,1)S(1)} collective-permute-done((bf16[32,4096]{1,0:T(8,128)(2,1)S(1)}, bf16[32,4096]{1,0:T(8,128)(2,1)S(1)}, u32[]{:S(2)}, u32[]{:S(2)}) %collective-permute-start.5) | collective-permute-done | bytes 262176 | tf_op jit(solution)/shard_map/ppermute | solution.py:19
  21.5 0.1 slice_add_fusion
  21.6 1.2 %collective-permute-start.6 = (bf16[16,4096]{1,0:T(8,128)(2,1)S(1)}, bf16[16,4096]{1,0:T(8,128)(2,1)S(1)}, u32[]{:S(2)}, u32[]{:S(2)}) collective-permute-start(bf16[16,4096]{1,0:T(8,128)(2,1)S(1)} %slice.83), channel_id=1, source_target_pairs={{0,2},{1,3},{2,0},{3,1},{4,6},{5,7},{6,4},{7,5},{8,10},{9,11},{10,... | collective-permute-start | bytes 393224 | tf_op jit(solution)/shard_map/ppermute | solution.py:19
  22.8 4.4 %collective-permute-done.6 = bf16[16,4096]{1,0:T(8,128)(2,1)S(1)} collective-permute-done((bf16[16,4096]{1,0:T(8,128)(2,1)S(1)}, bf16[16,4096]{1,0:T(8,128)(2,1)S(1)}, u32[]{:S(2)}, u32[]{:S(2)}) %collective-permute-start.6) | collective-permute-done | bytes 131104 | tf_op jit(solution)/shard_map/ppermute | solution.py:19
  27.3 0.7 %collective-permute-start.7 = (bf16[4,4096]{1,0:T(4,128)(2,1)S(1)}, bf16[4,4096]{1,0:T(4,128)(2,1)S(1)}, u32[]{:S(2)}, u32[]{:S(2)}) collective-permute-start(bf16[4,4096]{1,0:T(4,128)(2,1)S(1)} %get-tuple-element.22), channel_id=1, source_target_pairs={{0,8},{1,9},{2,10},{3,11},{4,12},{5,13},{6,14},{7,15},{8,0},{9,1},... | collective-permute-start | bytes 98312 | tf_op jit(solution)/shard_map/ppermute | solution.py:19
  28.0 3.6 %collective-permute-start.9 = (bf16[4,4096]{1,0:T(4,128)(2,1)S(1)}, bf16[4,4096]{1,0:T(4,128)(2,1)S(1)}, u32[]{:S(2)}, u32[]{:S(2)}) collective-permute-start(bf16[4,4096]{1,0:T(4,128)(2,1)S(1)} %get-tuple-element.23), channel_id=1, source_target_pairs={{0,12},{1,13},{2,14},{3,15},{4,8},{5,9},{6,10},{7,11},{8,4},{9,5},... | collective-permute-start | bytes 98312 | tf_op jit(solution)/shard_map/ppermute | solution.py:19
  31.6 0.0 collective-permute-start.8
  31.6 0.0 copy-done.3
  31.6 0.9 %collective-permute-done.7 = bf16[4,4096]{1,0:T(4,128)(2,1)S(1)} collective-permute-done((bf16[4,4096]{1,0:T(4,128)(2,1)S(1)}, bf16[4,4096]{1,0:T(4,128)(2,1)S(1)}, u32[]{:S(2)}, u32[]{:S(2)}) %collective-permute-start.7) | collective-permute-done | bytes 32800 | tf_op jit(solution)/shard_map/ppermute | solution.py:19
  32.5 1.3 %collective-permute-done.9 = bf16[4,4096]{1,0:T(4,128)(2,1)S(1)} collective-permute-done((bf16[4,4096]{1,0:T(4,128)(2,1)S(1)}, bf16[4,4096]{1,0:T(4,128)(2,1)S(1)}, u32[]{:S(2)}, u32[]{:S(2)}) %collective-permute-start.9) | collective-permute-done | bytes 32800 | tf_op jit(solution)/shard_map/ppermute | solution.py:19
  33.9 1.7 %collective-permute-done.8 = bf16[4,4096]{1,0:T(4,128)(2,1)S(1)} collective-permute-done((bf16[4,4096]{1,0:T(4,128)(2,1)S(1)}, bf16[4,4096]{1,0:T(4,128)(2,1)S(1)}, u32[]{:S(2)}, u32[]{:S(2)}) %collective-permute-start.8) | collective-permute-done | bytes 32800 | tf_op jit(solution)/shard_map/ppermute | solution.py:19
  35.6 0.1 fusion.11
  35.6 1.9 %collective-permute-start.12 = (bf16[4,4096]{1,0:T(4,128)(2,1)S(1)}, bf16[4,4096]{1,0:T(4,128)(2,1)S(1)}, u32[]{:S(2)}, u32[]{:S(2)}) collective-permute-start(bf16[4,4096]{1,0:T(4,128)(2,1)S(1)} %fusion.11), channel_id=1, source_target_pairs={{0,12},{1,13},{2,14},{3,15},{4,8},{5,9},{6,10},{7,11},{8,4},{9,5},... | collective-permute-start | bytes 98312 | tf_op jit(solution)/shard_map/ppermute | solution.py:19
  37.5 0.0 collective-permute-start.11
  37.5 2.6 %collective-permute-start.10 = (bf16[4,4096]{1,0:T(4,128)(2,1)S(1)}, bf16[4,4096]{1,0:T(4,128)(2,1)S(1)}, u32[]{:S(2)}, u32[]{:S(2)}) collective-permute-start(bf16[4,4096]{1,0:T(4,128)(2,1)S(1)} %fusion.11), channel_id=1, source_target_pairs={{0,8},{1,9},{2,10},{3,11},{4,12},{5,13},{6,14},{7,15},{8,0},{9,1},... | collective-permute-start | bytes 98312 | tf_op jit(solution)/shard_map/ppermute | solution.py:19
  40.1 1.4 %collective-permute-done.12 = bf16[4,4096]{1,0:T(4,128)(2,1)S(1)} collective-permute-done((bf16[4,4096]{1,0:T(4,128)(2,1)S(1)}, bf16[4,4096]{1,0:T(4,128)(2,1)S(1)}, u32[]{:S(2)}, u32[]{:S(2)}) %collective-permute-start.12) | collective-permute-done | bytes 32800 | tf_op jit(solution)/shard_map/ppermute | solution.py:19
  41.4 0.3 collective-permute-done.11
  41.7 0.6 collective-permute-done.10
  42.3 0.1 pad_maximum_fusion.2
  42.4 1.2 %collective-permute-start.13 = (bf16[16,4096]{1,0:T(8,128)(2,1)S(1)}, bf16[16,4096]{1,0:T(8,128)(2,1)S(1)}, u32[]{:S(2)}, u32[]{:S(2)}) collective-permute-start(bf16[16,4096]{1,0:T(8,128)(2,1)S(1)} %pad_maximum_fusion.2), channel_id=1, source_target_pairs={{0,2},{1,3},{2,0},{3,1},{4,6},{5,7},{6,4},{7,5},{8,10},{9,11},{10,... | collective-permute-start | bytes 393224 | tf_op jit(solution)/shard_map/ppermute | solution.py:19
  43.6 0.5 fusion.4
  44.1 3.3 %collective-permute-done.13 = bf16[16,4096]{1,0:T(8,128)(2,1)S(1)} collective-permute-done((bf16[16,4096]{1,0:T(8,128)(2,1)S(1)}, bf16[16,4096]{1,0:T(8,128)(2,1)S(1)}, u32[]{:S(2)}, u32[]{:S(2)}) %collective-permute-start.13) | collective-permute-done | bytes 131104 | tf_op jit(solution)/shard_map/ppermute | solution.py:19
  47.4 0.1 concatenate.25
  47.5 0.1 collective-permute-start.14
  47.6 0.7 %reshape.59 = bf16[4,2,2048]{2,1,0:T(2,128)(2,1)} reshape(bf16[4,4096]{1,0:T(4,128)(2,1)S(1)} %fusion.11) | data formatting | bytes 65536 | tf_op jit(solution)/shard_map/reshape | solution.py:97
  48.3 1.0 %collective-permute-done.14 = bf16[32,4096]{1,0:T(8,128)(2,1)} collective-permute-done((bf16[32,4096]{1,0:T(8,128)(2,1)S(1)}, bf16[32,4096]{1,0:T(8,128)(2,1)}, u32[]{:S(2)}, u32[]{:S(2)}) %collective-permute-start.14) | collective-permute-done | bytes 262176 | tf_op jit(solution)/shard_map/ppermute | solution.py:19
  49.3 1.1 %concatenate.26 = bf16[64,4096]{1,0:T(8,128)(2,1)S(1)} concatenate(bf16[4,4096]{1,0:T(4,128)(2,1)S(1)} %fusion.11, bf16[4,4096]{1,0:T(4,128)(2,1)S(1)} %collective-permute-done.10, bf16[4,4096]{1,0:T(4,128)(2,1)S(1)} %collective-permute-done.11, bf16[4,4096]{1,0:T(4,128)(2,1)S(1)} %collective-permute-done.12, bf16[16,4096]{1,0:T(8,128)(2,1)S(1)} %collective-permute-done.13, ...), dimensions={0} | concatenate | bytes 1048576 | tf_op jit(solution)/shard_map/concatenate | solution.py:32
  50.4 0.1 convert_reduce_fusion
  50.5 2.9 %convert_reduce_fusion.2 = (f32[256]{0:T(256)}, bf16[64,256]{1,0:T(8,128)(2,1)S(1)}) fusion(f32[256]{0:T(256)S(1)} %get-tuple-element.26, bf16[64,4096]{1,0:T(8,128)(2,1)S(1)} %concatenate.26, bf16[256,4096]{1,0:T(8,128)(2,1)} %bitcast.23, f32[64,256]{1,0:T(8,128)S(1)} %get-tuple-element.29), kind=kOutput, calls=%fused_computation.31 | convolution fusion | flops 134332160 | bytes 2721792 | tf_op jit(solution)/shard_map/dot_general | solution.py:80
  53.4 0.6 mul.92
  54.0 0.0 copy-start.2
  54.0 1.8 %fusion.3 = bf16[256,2048]{1,0:T(8,128)(2,1)S(1)} fusion(bf16[256,64]{0,1:T(8,128)(2,1)S(1)} %fusion.12, f32[256]{0:T(256)S(1)} %get-tuple-element.25, bf16[256,4096]{1,0:T(8,128)(2,1)} %bitcast.24, bf16[64,4096]{1,0:T(8,128)(2,1)S(1)} %concatenate.26), kind=kOutput, calls=%fused_computation.10 | convolution fusion | flops 69730304 | bytes 2393088 | tf_op jit(solution)/shard_map/dot_general | solution.py:89
  55.9 0.1 copy-done.2
  55.9 0.5 fusion.2
  56.4 0.2 pad_maximum_fusion
  56.6 3.5 %copy.10 = bf16[256,2,2048]{2,1,0:T(2,128)(2,1)} copy(bf16[256,2,2048]{2,0,1:T(8,128)(2,1)S(1)} %pad_maximum_fusion) | data formatting | bytes 4194304
  60.1 2.1 %convolution_convert_fusion = bf16[4096,256]{1,0:T(8,128)(2,1)} fusion(bf16[4096,64]{0,1:T(8,128)(2,1)S(1)} %bitcast.28, bf16[64,256]{1,0:T(8,128)(2,1)S(1)} %get-tuple-element.31), kind=kOutput, calls=%fused_computation | convolution fusion | flops 135266304 | bytes 2654208 | tf_op jit(solution)/shard_map/dot_general | solution.py:85
  (10 shorter events, 0.2 us)
Async XLA Ops:
  0.6 18.3 %copy-start = (bf16[2,2048,256]{2,1,0:T(8,128)(2,1)S(1)}, bf16[2,2048,256]{2,1,0:T(8,128)(2,1)}, u32[]{:S(2)}) copy-start(bf16[2,2048,256]{2,1,0:T(8,128)(2,1)} %param.6) | copy-start | bytes 6291460
  1.6 7.0 %collective-permute-start.2 = (bf16[4,4096]{1,0:T(4,128)(2,1)S(1)}, bf16[4,4096]{1,0:T(4,128)(2,1)S(1)}, u32[]{:S(2)}, u32[]{:S(2)}) collective-permute-start(bf16[4,4096]{1,0:T(4,128)(2,1)S(1)} %bitcast.33), channel_id=1, source_target_pairs={{0,12},{1,13},{2,14},{3,15},{4,8},{5,9},{6,10},{7,11},{8,4},{9,5},... | collective-permute-start | bytes 98312 | tf_op jit(solution)/shard_map/ppermute | solution.py:19
  6.7 3.9 %collective-permute-start.1 = (bf16[4,4096]{1,0:T(4,128)(2,1)S(1)}, bf16[4,4096]{1,0:T(4,128)(2,1)S(1)}, u32[]{:S(2)}, u32[]{:S(2)}) collective-permute-start(bf16[4,4096]{1,0:T(4,128)(2,1)S(1)} %bitcast.34), channel_id=1, source_target_pairs={{0,4},{1,5},{2,6},{3,7},{4,0},{5,1},{6,2},{7,3},{8,12},{9,13},{10,... | collective-permute-start | bytes 98312 | tf_op jit(solution)/shard_map/ppermute | solution.py:19
  6.7 4.9 %collective-permute-start = (bf16[4,4096]{1,0:T(4,128)(2,1)S(1)}, bf16[4,4096]{1,0:T(4,128)(2,1)S(1)}, u32[]{:S(2)}, u32[]{:S(2)}) collective-permute-start(bf16[4,4096]{1,0:T(4,128)(2,1)S(1)} %bitcast.35), channel_id=1, source_target_pairs={{0,8},{1,9},{2,10},{3,11},{4,12},{5,13},{6,14},{7,15},{8,0},{9,1},... | collective-permute-start | bytes 98312 | tf_op jit(solution)/shard_map/ppermute | solution.py:19
  11.7 5.4 %collective-permute-start.3 = (bf16[16,4096]{1,0:T(8,128)(2,1)S(1)}, bf16[16,4096]{1,0:T(8,128)(2,1)S(1)}, u32[]{:S(2)}, u32[]{:S(2)}) collective-permute-start(bf16[16,4096]{1,0:T(8,128)(2,1)S(1)} %pad_maximum_fusion.1), channel_id=1, source_target_pairs={{0,2},{1,3},{2,0},{3,1},{4,6},{5,7},{6,4},{7,5},{8,10},{9,11},{10,... | collective-permute-start | bytes 393224 | tf_op jit(solution)/shard_map/ppermute | solution.py:19
  13.3 5.6 %copy-start.4 = (f32[256]{0:T(256)S(1)}, f32[256]{0:T(256)}, u32[]{:S(2)}) copy-start(f32[256]{0:T(256)} %param.7) | copy-start | bytes 3076
  17.2 2.1 %copy-start.1 = (bf16[32,8,2,2048]{3,1,2,0:T(8,128)(2,1)S(1)}, bf16[32,8,2,2048]{3,1,2,0:T(8,128)(2,1)}, u32[]{:S(2)}) copy-start(bf16[32,8,2,2048]{3,1,2,0:T(8,128)(2,1)} %copy.12) | copy-start | bytes 6291460
  17.3 1.6 %collective-permute-start.4 = (bf16[32,4096]{1,0:T(8,128)(2,1)S(1)}, bf16[32,4096]{1,0:T(8,128)(2,1)S(1)}, u32[]{:S(2)}, u32[]{:S(2)}) collective-permute-start(bf16[32,4096]{1,0:T(8,128)(2,1)S(1)} %concatenate.22), channel_id=1, source_target_pairs={{0,1},{1,0},{2,3},{3,2},{4,5},{5,4},{6,7},{7,6},{8,9},{9,8},{10,11... | collective-permute-start | bytes 786440 | tf_op jit(solution)/shard_map/ppermute | solution.py:19
  19.9 11.8 %copy-start.3 = (f32[2,2048]{1,0:T(2,128)S(1)}, f32[2,2048]{1,0:T(2,128)}, u32[]{:S(2)}) copy-start(f32[2,2048]{1,0:T(2,128)} %param.9) | copy-start | bytes 49156
  19.9 1.6 %collective-permute-start.5 = (bf16[32,4096]{1,0:T(8,128)(2,1)S(1)}, bf16[32,4096]{1,0:T(8,128)(2,1)S(1)}, u32[]{:S(2)}, u32[]{:S(2)}) collective-permute-start(bf16[32,4096]{1,0:T(8,128)(2,1)S(1)} %slice.82), channel_id=1, source_target_pairs={{0,1},{1,0},{2,3},{3,2},{4,5},{5,4},{6,7},{7,6},{8,9},{9,8},{10,11... | collective-permute-start | bytes 786440 | tf_op jit(solution)/shard_map/ppermute | solution.py:19
  21.6 5.6 %collective-permute-start.6 = (bf16[16,4096]{1,0:T(8,128)(2,1)S(1)}, bf16[16,4096]{1,0:T(8,128)(2,1)S(1)}, u32[]{:S(2)}, u32[]{:S(2)}) collective-permute-start(bf16[16,4096]{1,0:T(8,128)(2,1)S(1)} %slice.83), channel_id=1, source_target_pairs={{0,2},{1,3},{2,0},{3,1},{4,6},{5,7},{6,4},{7,5},{8,10},{9,11},{10,... | collective-permute-start | bytes 393224 | tf_op jit(solution)/shard_map/ppermute | solution.py:19
  27.3 5.2 %collective-permute-start.7 = (bf16[4,4096]{1,0:T(4,128)(2,1)S(1)}, bf16[4,4096]{1,0:T(4,128)(2,1)S(1)}, u32[]{:S(2)}, u32[]{:S(2)}) collective-permute-start(bf16[4,4096]{1,0:T(4,128)(2,1)S(1)} %get-tuple-element.22), channel_id=1, source_target_pairs={{0,8},{1,9},{2,10},{3,11},{4,12},{5,13},{6,14},{7,15},{8,0},{9,1},... | collective-permute-start | bytes 98312 | tf_op jit(solution)/shard_map/ppermute | solution.py:19
  28.0 5.8 %collective-permute-start.9 = (bf16[4,4096]{1,0:T(4,128)(2,1)S(1)}, bf16[4,4096]{1,0:T(4,128)(2,1)S(1)}, u32[]{:S(2)}, u32[]{:S(2)}) collective-permute-start(bf16[4,4096]{1,0:T(4,128)(2,1)S(1)} %get-tuple-element.23), channel_id=1, source_target_pairs={{0,12},{1,13},{2,14},{3,15},{4,8},{5,9},{6,10},{7,11},{8,4},{9,5},... | collective-permute-start | bytes 98312 | tf_op jit(solution)/shard_map/ppermute | solution.py:19
  31.6 3.9 %collective-permute-start.8 = (bf16[4,4096]{1,0:T(4,128)(2,1)S(1)}, bf16[4,4096]{1,0:T(4,128)(2,1)S(1)}, u32[]{:S(2)}, u32[]{:S(2)}) collective-permute-start(bf16[4,4096]{1,0:T(4,128)(2,1)S(1)} %get-tuple-element.24), channel_id=1, source_target_pairs={{0,4},{1,5},{2,6},{3,7},{4,0},{5,1},{6,2},{7,3},{8,12},{9,13},{10,... | collective-permute-start | bytes 98312 | tf_op jit(solution)/shard_map/ppermute | solution.py:19
  35.6 5.8 %collective-permute-start.12 = (bf16[4,4096]{1,0:T(4,128)(2,1)S(1)}, bf16[4,4096]{1,0:T(4,128)(2,1)S(1)}, u32[]{:S(2)}, u32[]{:S(2)}) collective-permute-start(bf16[4,4096]{1,0:T(4,128)(2,1)S(1)} %fusion.11), channel_id=1, source_target_pairs={{0,12},{1,13},{2,14},{3,15},{4,8},{5,9},{6,10},{7,11},{8,4},{9,5},... | collective-permute-start | bytes 98312 | tf_op jit(solution)/shard_map/ppermute | solution.py:19
  37.5 4.3 %collective-permute-start.11 = (bf16[4,4096]{1,0:T(4,128)(2,1)S(1)}, bf16[4,4096]{1,0:T(4,128)(2,1)S(1)}, u32[]{:S(2)}, u32[]{:S(2)}) collective-permute-start(bf16[4,4096]{1,0:T(4,128)(2,1)S(1)} %fusion.11), channel_id=1, source_target_pairs={{0,4},{1,5},{2,6},{3,7},{4,0},{5,1},{6,2},{7,3},{8,12},{9,13},{10,... | collective-permute-start | bytes 98312 | tf_op jit(solution)/shard_map/ppermute | solution.py:19
  37.5 4.8 %collective-permute-start.10 = (bf16[4,4096]{1,0:T(4,128)(2,1)S(1)}, bf16[4,4096]{1,0:T(4,128)(2,1)S(1)}, u32[]{:S(2)}, u32[]{:S(2)}) collective-permute-start(bf16[4,4096]{1,0:T(4,128)(2,1)S(1)} %fusion.11), channel_id=1, source_target_pairs={{0,8},{1,9},{2,10},{3,11},{4,12},{5,13},{6,14},{7,15},{8,0},{9,1},... | collective-permute-start | bytes 98312 | tf_op jit(solution)/shard_map/ppermute | solution.py:19
  42.4 5.0 %collective-permute-start.13 = (bf16[16,4096]{1,0:T(8,128)(2,1)S(1)}, bf16[16,4096]{1,0:T(8,128)(2,1)S(1)}, u32[]{:S(2)}, u32[]{:S(2)}) collective-permute-start(bf16[16,4096]{1,0:T(8,128)(2,1)S(1)} %pad_maximum_fusion.2), channel_id=1, source_target_pairs={{0,2},{1,3},{2,0},{3,1},{4,6},{5,7},{6,4},{7,5},{8,10},{9,11},{10,... | collective-permute-start | bytes 393224 | tf_op jit(solution)/shard_map/ppermute | solution.py:19
  47.5 1.7 %collective-permute-start.14 = (bf16[32,4096]{1,0:T(8,128)(2,1)S(1)}, bf16[32,4096]{1,0:T(8,128)(2,1)}, u32[]{:S(2)}, u32[]{:S(2)}) collective-permute-start(bf16[32,4096]{1,0:T(8,128)(2,1)S(1)} %concatenate.25), channel_id=1, source_target_pairs={{0,1},{1,0},{2,3},{3,2},{4,5},{5,4},{6,7},{7,6},{8,9},{9,8},{10,11... | collective-permute-start | bytes 786440 | tf_op jit(solution)/shard_map/ppermute | solution.py:19
  54.0 1.9 %copy-start.2 = (bf16[32,8,2,2048]{3,1,2,0:T(8,128)(2,1)S(1)}, bf16[32,8,2,2048]{3,1,2,0:T(8,128)(2,1)}, u32[]{:S(2)}) copy-start(bf16[32,8,2,2048]{3,1,2,0:T(8,128)(2,1)} %copy.12) | copy-start | bytes 6291460

commit v3 on v1

--- a/solution.py
+++ b/solution.py
@@ -19,17 +19,38 @@
     return lax.ppermute(x, "lat", [(s, s ^ k) for s in range(count)])
 
 
-def gather_rows(x, count):
-    for k in masks_of(count):
-        x = jnp.concatenate([x, swap(x, k, count)], axis=0)
-    return x
+def steps_of(count):
+    masks = masks_of(count)
+    if len(masks) < 4:
+        return [[k] for k in masks]
+    return [[k] for k in masks[2:-1]] + [masks[:2], masks[-1:]]
 
 
-def scatter_rows(term, count):
-    for k in reversed(masks_of(count)):
-        half = term.shape[0] // 2
-        received = swap(term[half:].astype(jnp.bfloat16), k, count)
-        term = term[:half] + received.astype(jnp.float32)
+def gather_rows(x, count, direct, side=None):
+    for step in steps_of(count):
+        if side is not None and step == [1]:
+            x, side = lax.optimization_barrier((x, side))
+        if len(step) == 2:
+            far, near = step
+            others = [swap(x, k, count) for k in (far, near, far ^ near)]
+        else:
+            others = [swap(x, step[0], count)]
+        x = jnp.concatenate([x] + others, axis=0)
+    return x if side is None else (x, side)
+
+
+def scatter_rows(term, count, direct):
+    for step in reversed(steps_of(count)):
+        if len(step) == 2:
+            far, near = step
+            send = (far, near, far ^ near)
+        else:
+            send = (step[0],)
+        rows = term.shape[0] // (len(send) + 1)
+        got = [
+            swap(term[p * rows : (p + 1) * rows].astype(jnp.bfloat16), k, count) for p, k in enumerate(send, 1)
+        ]
+        term = term[:rows] + sum(g.astype(jnp.float32) for g in got)
     return term
 
 
@@ -44,13 +65,14 @@
     flat_enc = enc_weight.reshape(wide, lat_dev)
     flat_dec = lax.optimization_barrier(dec_weight.reshape(lat_dev, wide))
     flat_bias = dec_bias.reshape(wide)
-    gathered = gather_rows(flat_rows, count)
+    gathered, flat_dec = gather_rows(flat_rows, count, True, flat_dec)
     before = jnp.dot(gathered, flat_enc, preferred_element_type=jnp.float32) + enc_bias
     active = jnp.maximum(before, 0.0).astype(jnp.bfloat16)
     term = jnp.dot(active, flat_dec, preferred_element_type=jnp.float32)
-    summed = scatter_rows(term, count)
+    summed = scatter_rows(term, count, True)
     own_residual = (summed + flat_bias - flat_rows.astype(jnp.float32)).astype(jnp.bfloat16)
-    all_residual = gather_rows(own_residual, count)
+    own_residual, dec_t = lax.optimization_barrier((own_residual, flat_dec))
+    all_residual, dec_t = gather_rows(own_residual, count, True, lax.optimization_barrier(dec_t.T))
 
     layer_dec = [flat_dec[:, l * width : (l + 1) * width].astype(jnp.float32) for l in range(layers)]
     row_sq = [jnp.sum(d * d, axis=1) for d in layer_dec]
@@ -60,10 +82,14 @@
     active_t = lax.optimization_barrier(active.T)
     act_sum = jnp.sum(active.astype(jnp.float32), axis=0)
 
-    grad_dec_bias = factor * jnp.sum(all_residual.astype(jnp.float32), axis=0)
-    backward = lax.dot_general(
-        all_residual, flat_dec, (((1,), (1,)), ((), ())), preferred_element_type=jnp.float32
+    grad_dec_bias = jnp.concatenate(
+        [
+            factor * jnp.sum(all_residual[:, l * width : (l + 1) * width].astype(jnp.float32), axis=0, keepdims=True)
+            for l in range(layers)
+        ],
+        axis=0,
     )
+    backward = jnp.dot(all_residual, dec_t, preferred_element_type=jnp.float32)
     grad_act = factor * backward + sparsity_weight / total_rows * dec_norm
     grad_before = jnp.where(before > 0.0, grad_act, 0.0).astype(jnp.bfloat16)
     grad_enc = jnp.dot(gathered_t, grad_before, preferred_element_type=jnp.float32).astype(jnp.bfloat16)
@@ -82,7 +108,7 @@
         grad_enc.reshape(layers, width, lat_dev),
         grad_enc_bias,
         grad_dec,
-        grad_dec_bias.reshape(layers, width),
+        grad_dec_bias,
     )
 
 

time: 69.9 us -> 57.3 us (0.82)
  waiting for transfers between devices: 26.9 us -> 18.6 us
  local copies, waits for them, and re-layouts: 11.9 us -> 9.16 us
  matrix products: 8.25 us -> 6.53 us
    ppermute x12 -> x15, waiting for transfers between devices: 26.9 us -> 18.6 us  [swap(): return lax.ppermute(x, 'lat', [(s, s ^ k) for s in range(count)])]
    dot_general x1, matrix products: 2.93 us -> 1.34 us  [body(): backward = jnp.dot(all_residual, dec_t, preferred_element_type=jnp.float32)]
    unnamed x14 -> x16, local copies, waits for them, and re-layouts: 9.39 us -> 8.29 us
    concatenate x2 -> x4, local copies, waits for them, and re-layouts: 1.21 us -> 0.15 us  [gather_rows(): x = jnp.concatenate([x] + others, axis=0)]
    ppermute x12 -> x15, starting transfers between devices: 20.5 us -> 20.3 us  [swap(): return lax.ppermute(x, 'lat', [(s, s ^ k) for s in range(count)])]
  transfers between devices with their start and end apart: 12 -> 15, of which waited for: 11 -> 13; matrix products, arithmetic and copies ran while one was open for 7% -> 9% of each run, Pallas kernels for 0% -> 0%
where the time goes in v3:
time: 57.3 us; the launch traced here: 57.1 us
  starting transfers between devices  20.3 us (35%)
  waiting for transfers between devices  18.6 us (32%)
  local copies, waits for them, and re-layouts  9.16 us (16%)
  matrix products  6.53 us (11%)
  other arithmetic  1.63 us (3%)
  between operations  0.85 us (1%)
    ppermute x15, starting transfers between devices, swap(): return lax.ppermute(x, 'lat', [(s, s ^ k) for s in range(count)])  20.3 us
    ppermute x15, waiting for transfers between devices, swap(): return lax.ppermute(x, 'lat', [(s, s ^ k) for s in range(count)])  18.6 us
    unnamed x16, local copies, waits for them, and re-layouts  8.29 us
    dot_general x2, matrix products, body(): jnp.dot(active_t, all_residual[:, l * width:(l + 1) * width], preferred_e...  2.16 us
    dot_general x1, matrix products, body(): jnp.dot(gathered_t, grad_before, preferred_element_type=jnp.float32)  2.07 us
    dot_general x1, matrix products, body(): backward = jnp.dot(all_residual, dec_t, preferred_element_type=jnp.float32)  1.34 us
  transfers between devices with their start and end apart: 15, of which 13 were waited for; matrix products, arithmetic and copies ran while one was open for 9% of the time, Pallas kernels for 0%

profile of v3, /device:TPU:0, one launch (start us, length us, event | category | flops | bytes accessed | tf_op | source)
XLA Modules:
  0.0 57.1 jit_solution(4613107201247070088)
XLA Ops:
  0.6 0.0 copy-start
  0.6 0.9 %copy.11 = bf16[1,4,2,2048]{3,1,2,0:T(4,128)(2,1)S(1)} copy(bf16[1,4,2,2048]{3,2,1,0:T(2,128)(2,1)} %bitcast.41) | data formatting | bytes 65536
  1.6 3.1 %collective-permute-start = (bf16[4,4096]{1,0:T(4,128)(2,1)S(1)}, bf16[4,4096]{1,0:T(4,128)(2,1)S(1)}, u32[]{:S(2)}, u32[]{:S(2)}) collective-permute-start(bf16[4,4096]{1,0:T(4,128)(2,1)S(1)} %bitcast.36), channel_id=1, source_target_pairs={{0,2},{1,3},{2,0},{3,1},{4,6},{5,7},{6,4},{7,5},{8,10},{9,11},{10,... | collective-permute-start | bytes 98312 | tf_op jit(solution)/shard_map/ppermute | solution.py:19
  4.6 1.9 %collective-permute-done = bf16[4,4096]{1,0:T(4,128)(2,1)S(1)} collective-permute-done((bf16[4,4096]{1,0:T(4,128)(2,1)S(1)}, bf16[4,4096]{1,0:T(4,128)(2,1)S(1)}, u32[]{:S(2)}, u32[]{:S(2)}) %collective-permute-start) | collective-permute-done | bytes 32800 | tf_op jit(solution)/shard_map/ppermute | solution.py:19
  6.6 4.2 %collective-permute-start.3 = (bf16[8,4096]{1,0:T(8,128)(2,1)S(1)}, bf16[8,4096]{1,0:T(8,128)(2,1)S(1)}, u32[]{:S(2)}, u32[]{:S(2)}) collective-permute-start(bf16[8,4096]{1,0:T(8,128)(2,1)S(1)} %pad_maximum_fusion.1), channel_id=1, source_target_pairs={{0,12},{1,13},{2,14},{3,15},{4,8},{5,9},{6,10},{7,11},{8,4},{9,5},... | collective-permute-start | bytes 196616 | tf_op jit(solution)/shard_map/ppermute | solution.py:19
  10.7 0.0 collective-permute-start.2
  10.7 0.6 %collective-permute-start.1 = (bf16[8,4096]{1,0:T(8,128)(2,1)S(1)}, bf16[8,4096]{1,0:T(8,128)(2,1)S(1)}, u32[]{:S(2)}, u32[]{:S(2)}) collective-permute-start(bf16[8,4096]{1,0:T(8,128)(2,1)S(1)} %pad_maximum_fusion.1), channel_id=1, source_target_pairs={{0,8},{1,9},{2,10},{3,11},{4,12},{5,13},{6,14},{7,15},{8,0},{9,1},... | collective-permute-start | bytes 196616 | tf_op jit(solution)/shard_map/ppermute | solution.py:19
  11.4 0.0 copy-start.4
  11.4 3.8 %copy.12 = bf16[32,8,2,2048]{3,1,2,0:T(8,128)(2,1)} copy(bf16[32,8,2,2048]{3,2,1,0:T(2,128)(2,1)} %bitcast.32) | data formatting | bytes 4194304
  15.2 0.0 collective-permute-done.3
  15.2 0.0 collective-permute-done.2
  15.2 0.7 %collective-permute-done.1 = bf16[8,4096]{1,0:T(8,128)(2,1)S(1)} collective-permute-done((bf16[8,4096]{1,0:T(8,128)(2,1)S(1)}, bf16[8,4096]{1,0:T(8,128)(2,1)S(1)}, u32[]{:S(2)}, u32[]{:S(2)}) %collective-permute-start.1) | collective-permute-done | bytes 65568 | tf_op jit(solution)/shard_map/ppermute | solution.py:19
  15.9 0.1 concatenate.24
  16.0 0.0 copy-start.1
  16.0 0.1 collective-permute-start.4
  16.1 1.5 %collective-permute-done.4 = bf16[32,4096]{1,0:T(8,128)(2,1)S(1)} collective-permute-done((bf16[32,4096]{1,0:T(8,128)(2,1)S(1)}, bf16[32,4096]{1,0:T(8,128)(2,1)S(1)}, u32[]{:S(2)}, u32[]{:S(2)}) %collective-permute-start.4) | collective-permute-done | bytes 262176 | tf_op jit(solution)/shard_map/ppermute | solution.py:19
  17.6 0.0 copy-done
  17.6 0.0 copy-done.4
  17.6 0.5 convert_reduce_fusion.2
  18.1 0.0 copy-done.1
  18.1 0.0 copy-start.3
  18.1 0.5 fusion.13
  18.7 0.2 collective-permute-start.5
  18.9 1.4 %collective-permute-done.5 = bf16[32,4096]{1,0:T(8,128)(2,1)S(1)} collective-permute-done((bf16[32,4096]{1,0:T(8,128)(2,1)S(1)}, bf16[32,4096]{1,0:T(8,128)(2,1)S(1)}, u32[]{:S(2)}, u32[]{:S(2)}) %collective-permute-start.5) | collective-permute-done | bytes 262176 | tf_op jit(solution)/shard_map/ppermute | solution.py:19
  20.3 0.1 fusion.14
  20.3 1.7 %collective-permute-start.6 = (bf16[8,4096]{1,0:T(8,128)(2,1)S(1)}, bf16[8,4096]{1,0:T(8,128)(2,1)S(1)}, u32[]{:S(2)}, u32[]{:S(2)}) collective-permute-start(bf16[8,4096]{1,0:T(8,128)(2,1)S(1)} %get-tuple-element.32), channel_id=1, source_target_pairs={{0,8},{1,9},{2,10},{3,11},{4,12},{5,13},{6,14},{7,15},{8,0},{9,1},... | collective-permute-start | bytes 196616 | tf_op jit(solution)/shard_map/ppermute | solution.py:19
  22.0 2.8 %collective-permute-start.8 = (bf16[8,4096]{1,0:T(8,128)(2,1)S(1)}, bf16[8,4096]{1,0:T(8,128)(2,1)S(1)}, u32[]{:S(2)}, u32[]{:S(2)}) collective-permute-start(bf16[8,4096]{1,0:T(8,128)(2,1)S(1)} %get-tuple-element.33), channel_id=1, source_target_pairs={{0,12},{1,13},{2,14},{3,15},{4,8},{5,9},{6,10},{7,11},{8,4},{9,5},... | collective-permute-start | bytes 196616 | tf_op jit(solution)/shard_map/ppermute | solution.py:19
  24.8 0.0 collective-permute-start.7
  24.8 0.0 copy-done.3
  24.8 0.8 %collective-permute-done.6 = bf16[8,4096]{1,0:T(8,128)(2,1)S(1)} collective-permute-done((bf16[8,4096]{1,0:T(8,128)(2,1)S(1)}, bf16[8,4096]{1,0:T(8,128)(2,1)S(1)}, u32[]{:S(2)}, u32[]{:S(2)}) %collective-permute-start.6) | collective-permute-done | bytes 65568 | tf_op jit(solution)/shard_map/ppermute | solution.py:19
  25.6 3.6 %collective-permute-done.8 = bf16[8,4096]{1,0:T(8,128)(2,1)S(1)} collective-permute-done((bf16[8,4096]{1,0:T(8,128)(2,1)S(1)}, bf16[8,4096]{1,0:T(8,128)(2,1)S(1)}, u32[]{:S(2)}, u32[]{:S(2)}) %collective-permute-start.8) | collective-permute-done | bytes 65568 | tf_op jit(solution)/shard_map/ppermute | solution.py:19
  29.2 0.3 collective-permute-done.7
  29.5 1.6 %collective-permute-start.9 = (bf16[4,4096]{1,0:T(4,128)(2,1)S(1)}, bf16[4,4096]{1,0:T(4,128)(2,1)S(1)}, u32[]{:S(2)}, u32[]{:S(2)}) collective-permute-start(bf16[4,4096]{1,0:T(4,128)(2,1)S(1)} %slice.87), channel_id=1, source_target_pairs={{0,2},{1,3},{2,0},{3,1},{4,6},{5,7},{6,4},{7,5},{8,10},{9,11},{10,... | collective-permute-start | bytes 98312 | tf_op jit(solution)/shard_map/ppermute | solution.py:19
  31.1 0.5 fusion.4
  31.6 1.9 %collective-permute-done.9 = bf16[4,4096]{1,0:T(4,128)(2,1)S(1)} collective-permute-done((bf16[4,4096]{1,0:T(4,128)(2,1)S(1)}, bf16[4,4096]{1,0:T(4,128)(2,1)S(1)}, u32[]{:S(2)}, u32[]{:S(2)}) %collective-permute-start.9) | collective-permute-done | bytes 32800 | tf_op jit(solution)/shard_map/ppermute | solution.py:19
  33.5 1.6 %collective-permute-start.10 = (bf16[4,4096]{1,0:T(4,128)(2,1)S(1)}, bf16[4,4096]{1,0:T(4,128)(2,1)S(1)}, u32[]{:S(2)}, u32[]{:S(2)}) collective-permute-start(bf16[4,4096]{1,0:T(4,128)(2,1)S(1)} %fusion.11), channel_id=1, source_target_pairs={{0,2},{1,3},{2,0},{3,1},{4,6},{5,7},{6,4},{7,5},{8,10},{9,11},{10,... | collective-permute-start | bytes 98312 | tf_op jit(solution)/shard_map/ppermute | solution.py:19
  35.1 2.4 %collective-permute-done.10 = bf16[4,4096]{1,0:T(4,128)(2,1)S(1)} collective-permute-done((bf16[4,4096]{1,0:T(4,128)(2,1)S(1)}, bf16[4,4096]{1,0:T(4,128)(2,1)S(1)}, u32[]{:S(2)}, u32[]{:S(2)}) %collective-permute-start.10) | collective-permute-done | bytes 32800 | tf_op jit(solution)/shard_map/ppermute | solution.py:19
  37.6 2.7 %collective-permute-start.13 = (bf16[8,4096]{1,0:T(8,128)(2,1)S(1)}, bf16[8,4096]{1,0:T(8,128)(2,1)S(1)}, u32[]{:S(2)}, u32[]{:S(2)}) collective-permute-start(bf16[8,4096]{1,0:T(8,128)(2,1)S(1)} %pad_maximum_fusion.2), channel_id=1, source_target_pairs={{0,12},{1,13},{2,14},{3,15},{4,8},{5,9},{6,10},{7,11},{8,4},{9,5},... | collective-permute-start | bytes 196616 | tf_op jit(solution)/shard_map/ppermute | solution.py:19
  40.3 0.0 collective-permute-start.12
  40.3 1.8 %collective-permute-start.11 = (bf16[8,4096]{1,0:T(8,128)(2,1)S(1)}, bf16[8,4096]{1,0:T(8,128)(2,1)S(1)}, u32[]{:S(2)}, u32[]{:S(2)}) collective-permute-start(bf16[8,4096]{1,0:T(8,128)(2,1)S(1)} %pad_maximum_fusion.2), channel_id=1, source_target_pairs={{0,8},{1,9},{2,10},{3,11},{4,12},{5,13},{6,14},{7,15},{8,0},{9,1},... | collective-permute-start | bytes 196616 | tf_op jit(solution)/shard_map/ppermute | solution.py:19
  42.0 0.7 %reshape.75 = bf16[4,2,2048]{2,1,0:T(2,128)(2,1)} reshape(bf16[4,4096]{1,0:T(4,128)(2,1)S(1)} %fusion.11) | data formatting | bytes 65536 | tf_op jit(solution)/shard_map/reshape | solution.py:107
  42.7 1.1 %collective-permute-done.13 = bf16[8,4096]{1,0:T(8,128)(2,1)S(1)} collective-permute-done((bf16[8,4096]{1,0:T(8,128)(2,1)S(1)}, bf16[8,4096]{1,0:T(8,128)(2,1)S(1)}, u32[]{:S(2)}, u32[]{:S(2)}) %collective-permute-start.13) | collective-permute-done | bytes 65568 | tf_op jit(solution)/shard_map/ppermute | solution.py:19
  43.8 0.7 %collective-permute-done.12 = bf16[8,4096]{1,0:T(8,128)(2,1)S(1)} collective-permute-done((bf16[8,4096]{1,0:T(8,128)(2,1)S(1)}, bf16[8,4096]{1,0:T(8,128)(2,1)S(1)}, u32[]{:S(2)}, u32[]{:S(2)}) %collective-permute-start.12) | collective-permute-done | bytes 65568 | tf_op jit(solution)/shard_map/ppermute | solution.py:19
  44.5 0.9 %collective-permute-done.11 = bf16[8,4096]{1,0:T(8,128)(2,1)S(1)} collective-permute-done((bf16[8,4096]{1,0:T(8,128)(2,1)S(1)}, bf16[8,4096]{1,0:T(8,128)(2,1)S(1)}, u32[]{:S(2)}, u32[]{:S(2)}) %collective-permute-start.11) | collective-permute-done | bytes 65568 | tf_op jit(solution)/shard_map/ppermute | solution.py:19
  45.4 0.1 concatenate.27
  45.5 0.1 collective-permute-start.14
  45.6 0.0 copy-start.2
  45.6 1.5 %collective-permute-done.14 = bf16[32,4096]{1,0:T(8,128)(2,1)S(1)} collective-permute-done((bf16[32,4096]{1,0:T(8,128)(2,1)S(1)}, bf16[32,4096]{1,0:T(8,128)(2,1)S(1)}, u32[]{:S(2)}, u32[]{:S(2)}) %collective-permute-start.14) | collective-permute-done | bytes 262176 | tf_op jit(solution)/shard_map/ppermute | solution.py:19
  47.1 0.1 convert_reduce_fusion.1
  47.2 1.7 %fusion.3 = bf16[256,2048]{1,0:T(8,128)(2,1)S(1)} fusion(bf16[256,64]{0,1:T(8,128)(2,1)S(1)} %fusion.12, f32[256]{0:T(256)S(1)} %get-tuple-element.35, bf16[256,4096]{1,0:T(8,128)(2,1)} %bitcast.26, bf16[64,4096]{1,0:T(8,128)(2,1)S(1)} %constant_dynamic-update-slice_fusion.2), kind=kOutput, calls=%fused_computation.10 | convolution fusion | flops 69730304 | bytes 2393088 | tf_op jit(solution)/shard_map/dot_general | solution.py:99
  48.9 0.0 copy-done.2
  48.9 0.5 fusion.2
  49.4 0.2 pad_maximum_fusion
  49.6 3.5 %copy.10 = bf16[256,2,2048]{2,1,0:T(2,128)(2,1)} copy(bf16[256,2,2048]{2,0,1:T(8,128)(2,1)S(1)} %pad_maximum_fusion) | data formatting | bytes 4194304
  53.1 1.3 %convert_reduce_fusion.3 = (f32[256]{0:T(256)}, bf16[64,256]{1,0:T(8,128)(2,1)S(1)}) fusion(f32[256]{0:T(256)S(1)} %get-tuple-element.36, bf16[64,4096]{1,0:T(8,128)(2,1)S(1)} %constant_dynamic-update-slice_fusion.2, bf16[4096,256]{0,1:T(8,128)(2,1)S(1)} %bitcast.30, f32[64,256]{1,0:T(8,128)S(1)} %get-tuple-element.39), kind=kOutput, calls=%fused_computation.32 | convolution fusion | flops 134332160 | bytes 2721792 | tf_op jit(solution)/shard_map/dot_general | solution.py:92
  54.4 0.6 %pad_maximum_fusion.3 = f32[2,2048]{1,0:T(2,128)} fusion(f32[1,2048]{1,0:T(1,128)S(1)} %bitcast.42, f32[1,2048]{1,0:T(1,128)S(1)} %bitcast.43), kind=kLoop, calls=%fused_computation.35 | loop fusion | flops 4096 | bytes 32768 | tf_op jit(solution)/shard_map/concatenate | solution.py:85
  55.1 2.1 %convolution_convert_fusion = bf16[4096,256]{1,0:T(8,128)(2,1)} fusion(bf16[4096,64]{0,1:T(8,128)(2,1)S(1)} %bitcast.31, bf16[64,256]{1,0:T(8,128)(2,1)S(1)} %get-tuple-element.41), kind=kOutput, calls=%fused_computation | convolution fusion | flops 135266304 | bytes 2654208 | tf_op jit(solution)/shard_map/dot_general | solution.py:95
  (15 shorter events, 0.3 us)
Async XLA Ops:
  0.6 17.0 %copy-start = (bf16[2,2048,256]{2,1,0:T(8,128)(2,1)S(1)}, bf16[2,2048,256]{2,1,0:T(8,128)(2,1)}, u32[]{:S(2)}) copy-start(bf16[2,2048,256]{2,1,0:T(8,128)(2,1)} %param.6) | copy-start | bytes 6291460
  1.6 5.0 %collective-permute-start = (bf16[4,4096]{1,0:T(4,128)(2,1)S(1)}, bf16[4,4096]{1,0:T(4,128)(2,1)S(1)}, u32[]{:S(2)}, u32[]{:S(2)}) collective-permute-start(bf16[4,4096]{1,0:T(4,128)(2,1)S(1)} %bitcast.36), channel_id=1, source_target_pairs={{0,2},{1,3},{2,0},{3,1},{4,6},{5,7},{6,4},{7,5},{8,10},{9,11},{10,... | collective-permute-start | bytes 98312 | tf_op jit(solution)/shard_map/ppermute | solution.py:19
  6.6 8.6 %collective-permute-start.3 = (bf16[8,4096]{1,0:T(8,128)(2,1)S(1)}, bf16[8,4096]{1,0:T(8,128)(2,1)S(1)}, u32[]{:S(2)}, u32[]{:S(2)}) collective-permute-start(bf16[8,4096]{1,0:T(8,128)(2,1)S(1)} %pad_maximum_fusion.1), channel_id=1, source_target_pairs={{0,12},{1,13},{2,14},{3,15},{4,8},{5,9},{6,10},{7,11},{8,4},{9,5},... | collective-permute-start | bytes 196616 | tf_op jit(solution)/shard_map/ppermute | solution.py:19
  10.7 4.5 %collective-permute-start.2 = (bf16[8,4096]{1,0:T(8,128)(2,1)S(1)}, bf16[8,4096]{1,0:T(8,128)(2,1)S(1)}, u32[]{:S(2)}, u32[]{:S(2)}) collective-permute-start(bf16[8,4096]{1,0:T(8,128)(2,1)S(1)} %pad_maximum_fusion.1), channel_id=1, source_target_pairs={{0,4},{1,5},{2,6},{3,7},{4,0},{5,1},{6,2},{7,3},{8,12},{9,13},{10,... | collective-permute-start | bytes 196616 | tf_op jit(solution)/shard_map/ppermute | solution.py:19
  10.7 5.2 %collective-permute-start.1 = (bf16[8,4096]{1,0:T(8,128)(2,1)S(1)}, bf16[8,4096]{1,0:T(8,128)(2,1)S(1)}, u32[]{:S(2)}, u32[]{:S(2)}) collective-permute-start(bf16[8,4096]{1,0:T(8,128)(2,1)S(1)} %pad_maximum_fusion.1), channel_id=1, source_target_pairs={{0,8},{1,9},{2,10},{3,11},{4,12},{5,13},{6,14},{7,15},{8,0},{9,1},... | collective-permute-start | bytes 196616 | tf_op jit(solution)/shard_map/ppermute | solution.py:19
  11.4 6.2 %copy-start.4 = (f32[256]{0:T(256)S(1)}, f32[256]{0:T(256)}, u32[]{:S(2)}) copy-start(f32[256]{0:T(256)} %param.7) | copy-start | bytes 3076
  16.0 2.1 %copy-start.1 = (bf16[32,8,2,2048]{3,1,2,0:T(8,128)(2,1)S(1)}, bf16[32,8,2,2048]{3,1,2,0:T(8,128)(2,1)}, u32[]{:S(2)}) copy-start(bf16[32,8,2,2048]{3,1,2,0:T(8,128)(2,1)} %copy.12) | copy-start | bytes 6291460
  16.0 1.6 %collective-permute-start.4 = (bf16[32,4096]{1,0:T(8,128)(2,1)S(1)}, bf16[32,4096]{1,0:T(8,128)(2,1)S(1)}, u32[]{:S(2)}, u32[]{:S(2)}) collective-permute-start(bf16[32,4096]{1,0:T(8,128)(2,1)S(1)} %concatenate.24), channel_id=1, source_target_pairs={{0,1},{1,0},{2,3},{3,2},{4,5},{5,4},{6,7},{7,6},{8,9},{9,8},{10,11... | collective-permute-start | bytes 786440 | tf_op jit(solution)/shard_map/ppermute | solution.py:19
  18.1 6.7 %copy-start.3 = (f32[2,2048]{1,0:T(2,128)S(1)}, f32[2,2048]{1,0:T(2,128)}, u32[]{:S(2)}) copy-start(f32[2,2048]{1,0:T(2,128)} %param.9) | copy-start | bytes 49156
  18.7 1.6 %collective-permute-start.5 = (bf16[32,4096]{1,0:T(8,128)(2,1)S(1)}, bf16[32,4096]{1,0:T(8,128)(2,1)S(1)}, u32[]{:S(2)}, u32[]{:S(2)}) collective-permute-start(bf16[32,4096]{1,0:T(8,128)(2,1)S(1)} %slice.86), channel_id=1, source_target_pairs={{0,1},{1,0},{2,3},{3,2},{4,5},{5,4},{6,7},{7,6},{8,9},{9,8},{10,11... | collective-permute-start | bytes 786440 | tf_op jit(solution)/shard_map/ppermute | solution.py:19
  20.3 5.2 %collective-permute-start.6 = (bf16[8,4096]{1,0:T(8,128)(2,1)S(1)}, bf16[8,4096]{1,0:T(8,128)(2,1)S(1)}, u32[]{:S(2)}, u32[]{:S(2)}) collective-permute-start(bf16[8,4096]{1,0:T(8,128)(2,1)S(1)} %get-tuple-element.32), channel_id=1, source_target_pairs={{0,8},{1,9},{2,10},{3,11},{4,12},{5,13},{6,14},{7,15},{8,0},{9,1},... | collective-permute-start | bytes 196616 | tf_op jit(solution)/shard_map/ppermute | solution.py:19
  22.0 7.2 %collective-permute-start.8 = (bf16[8,4096]{1,0:T(8,128)(2,1)S(1)}, bf16[8,4096]{1,0:T(8,128)(2,1)S(1)}, u32[]{:S(2)}, u32[]{:S(2)}) collective-permute-start(bf16[8,4096]{1,0:T(8,128)(2,1)S(1)} %get-tuple-element.33), channel_id=1, source_target_pairs={{0,12},{1,13},{2,14},{3,15},{4,8},{5,9},{6,10},{7,11},{8,4},{9,5},... | collective-permute-start | bytes 196616 | tf_op jit(solution)/shard_map/ppermute | solution.py:19
  24.8 4.7 %collective-permute-start.7 = (bf16[8,4096]{1,0:T(8,128)(2,1)S(1)}, bf16[8,4096]{1,0:T(8,128)(2,1)S(1)}, u32[]{:S(2)}, u32[]{:S(2)}) collective-permute-start(bf16[8,4096]{1,0:T(8,128)(2,1)S(1)} %get-tuple-element.34), channel_id=1, source_target_pairs={{0,4},{1,5},{2,6},{3,7},{4,0},{5,1},{6,2},{7,3},{8,12},{9,13},{10,... | collective-permute-start | bytes 196616 | tf_op jit(solution)/shard_map/ppermute | solution.py:19
  29.5 4.0 %collective-permute-start.9 = (bf16[4,4096]{1,0:T(4,128)(2,1)S(1)}, bf16[4,4096]{1,0:T(4,128)(2,1)S(1)}, u32[]{:S(2)}, u32[]{:S(2)}) collective-permute-start(bf16[4,4096]{1,0:T(4,128)(2,1)S(1)} %slice.87), channel_id=1, source_target_pairs={{0,2},{1,3},{2,0},{3,1},{4,6},{5,7},{6,4},{7,5},{8,10},{9,11},{10,... | collective-permute-start | bytes 98312 | tf_op jit(solution)/shard_map/ppermute | solution.py:19
  33.5 4.0 %collective-permute-start.10 = (bf16[4,4096]{1,0:T(4,128)(2,1)S(1)}, bf16[4,4096]{1,0:T(4,128)(2,1)S(1)}, u32[]{:S(2)}, u32[]{:S(2)}) collective-permute-start(bf16[4,4096]{1,0:T(4,128)(2,1)S(1)} %fusion.11), channel_id=1, source_target_pairs={{0,2},{1,3},{2,0},{3,1},{4,6},{5,7},{6,4},{7,5},{8,10},{9,11},{10,... | collective-permute-start | bytes 98312 | tf_op jit(solution)/shard_map/ppermute | solution.py:19
  37.6 6.2 %collective-permute-start.13 = (bf16[8,4096]{1,0:T(8,128)(2,1)S(1)}, bf16[8,4096]{1,0:T(8,128)(2,1)S(1)}, u32[]{:S(2)}, u32[]{:S(2)}) collective-permute-start(bf16[8,4096]{1,0:T(8,128)(2,1)S(1)} %pad_maximum_fusion.2), channel_id=1, source_target_pairs={{0,12},{1,13},{2,14},{3,15},{4,8},{5,9},{6,10},{7,11},{8,4},{9,5},... | collective-permute-start | bytes 196616 | tf_op jit(solution)/shard_map/ppermute | solution.py:19
  40.3 4.3 %collective-permute-start.12 = (bf16[8,4096]{1,0:T(8,128)(2,1)S(1)}, bf16[8,4096]{1,0:T(8,128)(2,1)S(1)}, u32[]{:S(2)}, u32[]{:S(2)}) collective-permute-start(bf16[8,4096]{1,0:T(8,128)(2,1)S(1)} %pad_maximum_fusion.2), channel_id=1, source_target_pairs={{0,4},{1,5},{2,6},{3,7},{4,0},{5,1},{6,2},{7,3},{8,12},{9,13},{10,... | collective-permute-start | bytes 196616 | tf_op jit(solution)/shard_map/ppermute | solution.py:19
  40.3 5.2 %collective-permute-start.11 = (bf16[8,4096]{1,0:T(8,128)(2,1)S(1)}, bf16[8,4096]{1,0:T(8,128)(2,1)S(1)}, u32[]{:S(2)}, u32[]{:S(2)}) collective-permute-start(bf16[8,4096]{1,0:T(8,128)(2,1)S(1)} %pad_maximum_fusion.2), channel_id=1, source_target_pairs={{0,8},{1,9},{2,10},{3,11},{4,12},{5,13},{6,14},{7,15},{8,0},{9,1},... | collective-permute-start | bytes 196616 | tf_op jit(solution)/shard_map/ppermute | solution.py:19
  45.5 1.6 %collective-permute-start.14 = (bf16[32,4096]{1,0:T(8,128)(2,1)S(1)}, bf16[32,4096]{1,0:T(8,128)(2,1)S(1)}, u32[]{:S(2)}, u32[]{:S(2)}) collective-permute-start(bf16[32,4096]{1,0:T(8,128)(2,1)S(1)} %concatenate.27), channel_id=1, source_target_pairs={{0,1},{1,0},{2,3},{3,2},{4,5},{5,4},{6,7},{7,6},{8,9},{9,8},{10,11... | collective-permute-start | bytes 786440 | tf_op jit(solution)/shard_map/ppermute | solution.py:19
  45.6 3.3 %copy-start.2 = (bf16[32,8,2,2048]{3,1,2,0:T(8,128)(2,1)S(1)}, bf16[32,8,2,2048]{3,1,2,0:T(8,128)(2,1)}, u32[]{:S(2)}) copy-start(bf16[32,8,2,2048]{3,1,2,0:T(8,128)(2,1)} %copy.12) | copy-start | bytes 6291460

commit v4 on v3

--- a/solution.py
+++ b/solution.py
@@ -26,9 +26,9 @@
     return [[k] for k in masks[2:-1]] + [masks[:2], masks[-1:]]
 
 
-def gather_rows(x, count, direct, side=None):
+def gather_rows(x, count, direct, side=None, side_at=2):
     for step in steps_of(count):
-        if side is not None and step == [1]:
+        if side is not None and len(step) == side_at:
             x, side = lax.optimization_barrier((x, side))
         if len(step) == 2:
             far, near = step
@@ -72,7 +72,7 @@
     summed = scatter_rows(term, count, True)
     own_residual = (summed + flat_bias - flat_rows.astype(jnp.float32)).astype(jnp.bfloat16)
     own_residual, dec_t = lax.optimization_barrier((own_residual, flat_dec))
-    all_residual, dec_t = gather_rows(own_residual, count, True, lax.optimization_barrier(dec_t.T))
+    all_residual, dec_t = gather_rows(own_residual, count, True, lax.optimization_barrier(dec_t.T), 1)
 
     layer_dec = [flat_dec[:, l * width : (l + 1) * width].astype(jnp.float32) for l in range(layers)]
     row_sq = [jnp.sum(d * d, axis=1) for d in layer_dec]

time: 57.3 us -> 58 us (1.012)
  waiting for transfers between devices: 18.6 us -> 22.3 us
  starting transfers between devices: 20.3 us -> 18.7 us
  local copies, waits for them, and re-layouts: 9.16 us -> 7.79 us
    ppermute x15, waiting for transfers between devices: 18.6 us -> 22.3 us  [swap(): return lax.ppermute(x, 'lat', [(s, s ^ k) for s in range(count)])]
    ppermute x15, starting transfers between devices: 20.3 us -> 18.7 us  [swap(): return lax.ppermute(x, 'lat', [(s, s ^ k) for s in range(count)])]
    unnamed x16 -> x19, local copies, waits for them, and re-layouts: 8.29 us -> 6.98 us
  transfers between devices with their start and end apart: 15 -> 15, of which waited for: 13 -> 14; matrix products, arithmetic and copies ran while one was open for 9% -> 6% of each run, Pallas kernels for 0% -> 0%
where the time goes in v4:
time: 58 us; the launch traced here: 57.8 us
  waiting for transfers between devices  22.3 us (38%)
  starting transfers between devices  18.7 us (32%)
  local copies, waits for them, and re-layouts  7.79 us (13%)
  matrix products  6.52 us (11%)
  other arithmetic  1.65 us (3%)
  between operations  0.87 us (2%)
    ppermute x15, waiting for transfers between devices, swap(): return lax.ppermute(x, 'lat', [(s, s ^ k) for s in range(count)])  22.3 us
    ppermute x15, starting transfers between devices, swap(): return lax.ppermute(x, 'lat', [(s, s ^ k) for s in range(count)])  18.7 us
    unnamed x19, local copies, waits for them, and re-layouts  6.98 us
    dot_general x2, matrix products, body(): jnp.dot(active_t, all_residual[:, l * width:(l + 1) * width], preferred_e...  2.16 us
    dot_general x1, matrix products, body(): jnp.dot(gathered_t, grad_before, preferred_element_type=jnp.float32)  2.07 us
    dot_general x1, matrix products, body(): backward = jnp.dot(all_residual, dec_t, preferred_element_type=jnp.float32)  1.34 us
  transfers between devices with their start and end apart: 15, of which 14 were waited for; matrix products, arithmetic and copies ran while one was open for 6% of the time, Pallas kernels for 0%

profile of v4, /device:TPU:0, one launch (start us, length us, event | category | flops | bytes accessed | tf_op | source)
XLA Modules:
  0.0 57.8 jit_solution(11559038508787522867)
XLA Ops:
  0.6 0.0 copy-start
  0.6 0.9 %copy.11 = bf16[1,4,2,2048]{3,1,2,0:T(4,128)(2,1)S(1)} copy(bf16[1,4,2,2048]{3,2,1,0:T(2,128)(2,1)} %bitcast.40) | data formatting | bytes 65536
  1.6 3.1 %collective-permute-start = (bf16[4,4096]{1,0:T(4,128)(2,1)S(1)}, bf16[4,4096]{1,0:T(4,128)(2,1)S(1)}, u32[]{:S(2)}, u32[]{:S(2)}) collective-permute-start(bf16[4,4096]{1,0:T(4,128)(2,1)S(1)} %bitcast.36), channel_id=1, source_target_pairs={{0,2},{1,3},{2,0},{3,1},{4,6},{5,7},{6,4},{7,5},{8,10},{9,11},{10,... | collective-permute-start | bytes 98312 | tf_op jit(solution)/shard_map/ppermute | solution.py:19
  4.6 0.0 copy-start.4
  4.6 2.5 %copy.12 = bf16[32,8,2,2048]{3,1,2,0:T(8,128)(2,1)S(1)} copy(bf16[32,8,2,2048]{3,2,1,0:T(2,128)(2,1)} %bitcast.32) | data formatting | bytes 4194304
  7.1 0.0 copy-start.1
  7.1 0.0 collective-permute-done
  7.2 3.7 %collective-permute-start.3 = (bf16[8,4096]{1,0:T(8,128)(2,1)S(1)}, bf16[8,4096]{1,0:T(8,128)(2,1)S(1)}, u32[]{:S(2)}, u32[]{:S(2)}) collective-permute-start(bf16[8,4096]{1,0:T(8,128)(2,1)S(1)} %pad_maximum_fusion.2), channel_id=1, source_target_pairs={{0,12},{1,13},{2,14},{3,15},{4,8},{5,9},{6,10},{7,11},{8,4},{9,5},... | collective-permute-start | bytes 196616 | tf_op jit(solution)/shard_map/ppermute | solution.py:19
  10.9 0.0 collective-permute-start.2
  10.9 0.8 %collective-permute-start.1 = (bf16[8,4096]{1,0:T(8,128)(2,1)S(1)}, bf16[8,4096]{1,0:T(8,128)(2,1)S(1)}, u32[]{:S(2)}, u32[]{:S(2)}) collective-permute-start(bf16[8,4096]{1,0:T(8,128)(2,1)S(1)} %pad_maximum_fusion.2), channel_id=1, source_target_pairs={{0,8},{1,9},{2,10},{3,11},{4,12},{5,13},{6,14},{7,15},{8,0},{9,1},... | collective-permute-start | bytes 196616 | tf_op jit(solution)/shard_map/ppermute | solution.py:19
  11.7 1.8 %collective-permute-done.3 = bf16[8,4096]{1,0:T(8,128)(2,1)S(1)} collective-permute-done((bf16[8,4096]{1,0:T(8,128)(2,1)S(1)}, bf16[8,4096]{1,0:T(8,128)(2,1)S(1)}, u32[]{:S(2)}, u32[]{:S(2)}) %collective-permute-start.3) | collective-permute-done | bytes 65568 | tf_op jit(solution)/shard_map/ppermute | solution.py:19
  13.5 2.1 %collective-permute-done.2 = bf16[8,4096]{1,0:T(8,128)(2,1)S(1)} collective-permute-done((bf16[8,4096]{1,0:T(8,128)(2,1)S(1)}, bf16[8,4096]{1,0:T(8,128)(2,1)S(1)}, u32[]{:S(2)}, u32[]{:S(2)}) %collective-permute-start.2) | collective-permute-done | bytes 65568 | tf_op jit(solution)/shard_map/ppermute | solution.py:19
  15.5 0.7 %collective-permute-done.1 = bf16[8,4096]{1,0:T(8,128)(2,1)S(1)} collective-permute-done((bf16[8,4096]{1,0:T(8,128)(2,1)S(1)}, bf16[8,4096]{1,0:T(8,128)(2,1)S(1)}, u32[]{:S(2)}, u32[]{:S(2)}) %collective-permute-start.1) | collective-permute-done | bytes 65568 | tf_op jit(solution)/shard_map/ppermute | solution.py:19
  16.2 0.1 collective-permute-start.4
  16.4 1.5 %collective-permute-done.4 = bf16[32,4096]{1,0:T(8,128)(2,1)S(1)} collective-permute-done((bf16[32,4096]{1,0:T(8,128)(2,1)S(1)}, bf16[32,4096]{1,0:T(8,128)(2,1)S(1)}, u32[]{:S(2)}, u32[]{:S(2)}) %collective-permute-start.4) | collective-permute-done | bytes 262176 | tf_op jit(solution)/shard_map/ppermute | solution.py:19
  17.9 0.0 copy-done
  17.9 0.0 copy-done.4
  17.9 0.5 convert_reduce_fusion.2
  18.4 0.0 copy-start.3
  18.4 0.5 fusion.13
  18.9 0.2 collective-permute-start.5
  19.1 1.4 %collective-permute-done.5 = bf16[32,4096]{1,0:T(8,128)(2,1)S(1)} collective-permute-done((bf16[32,4096]{1,0:T(8,128)(2,1)S(1)}, bf16[32,4096]{1,0:T(8,128)(2,1)S(1)}, u32[]{:S(2)}, u32[]{:S(2)}) %collective-permute-start.5) | collective-permute-done | bytes 262176 | tf_op jit(solution)/shard_map/ppermute | solution.py:19
  20.5 0.1 fusion.14
  20.6 2.1 %collective-permute-start.6 = (bf16[8,4096]{1,0:T(8,128)(2,1)S(1)}, bf16[8,4096]{1,0:T(8,128)(2,1)S(1)}, u32[]{:S(2)}, u32[]{:S(2)}) collective-permute-start(bf16[8,4096]{1,0:T(8,128)(2,1)S(1)} %get-tuple-element.36), channel_id=1, source_target_pairs={{0,8},{1,9},{2,10},{3,11},{4,12},{5,13},{6,14},{7,15},{8,0},{9,1},... | collective-permute-start | bytes 196616 | tf_op jit(solution)/shard_map/ppermute | solution.py:19
  22.7 2.1 %collective-permute-start.8 = (bf16[8,4096]{1,0:T(8,128)(2,1)S(1)}, bf16[8,4096]{1,0:T(8,128)(2,1)S(1)}, u32[]{:S(2)}, u32[]{:S(2)}) collective-permute-start(bf16[8,4096]{1,0:T(8,128)(2,1)S(1)} %get-tuple-element.37), channel_id=1, source_target_pairs={{0,12},{1,13},{2,14},{3,15},{4,8},{5,9},{6,10},{7,11},{8,4},{9,5},... | collective-permute-start | bytes 196616 | tf_op jit(solution)/shard_map/ppermute | solution.py:19
  24.9 0.0 collective-permute-start.7
  24.9 0.0 copy-done.3
  24.9 3.2 %collective-permute-done.6 = bf16[8,4096]{1,0:T(8,128)(2,1)S(1)} collective-permute-done((bf16[8,4096]{1,0:T(8,128)(2,1)S(1)}, bf16[8,4096]{1,0:T(8,128)(2,1)S(1)}, u32[]{:S(2)}, u32[]{:S(2)}) %collective-permute-start.6) | collective-permute-done | bytes 65568 | tf_op jit(solution)/shard_map/ppermute | solution.py:19
  28.1 1.1 %collective-permute-done.8 = bf16[8,4096]{1,0:T(8,128)(2,1)S(1)} collective-permute-done((bf16[8,4096]{1,0:T(8,128)(2,1)S(1)}, bf16[8,4096]{1,0:T(8,128)(2,1)S(1)}, u32[]{:S(2)}, u32[]{:S(2)}) %collective-permute-start.8) | collective-permute-done | bytes 65568 | tf_op jit(solution)/shard_map/ppermute | solution.py:19
  29.2 0.7 %collective-permute-done.7 = bf16[8,4096]{1,0:T(8,128)(2,1)S(1)} collective-permute-done((bf16[8,4096]{1,0:T(8,128)(2,1)S(1)}, bf16[8,4096]{1,0:T(8,128)(2,1)S(1)}, u32[]{:S(2)}, u32[]{:S(2)}) %collective-permute-start.7) | collective-permute-done | bytes 65568 | tf_op jit(solution)/shard_map/ppermute | solution.py:19
  30.0 1.0 %collective-permute-start.9 = (bf16[4,4096]{1,0:T(4,128)(2,1)S(1)}, bf16[4,4096]{1,0:T(4,128)(2,1)S(1)}, u32[]{:S(2)}, u32[]{:S(2)}) collective-permute-start(bf16[4,4096]{1,0:T(4,128)(2,1)S(1)} %slice.87), channel_id=1, source_target_pairs={{0,2},{1,3},{2,0},{3,1},{4,6},{5,7},{6,4},{7,5},{8,10},{9,11},{10,... | collective-permute-start | bytes 98312 | tf_op jit(solution)/shard_map/ppermute | solution.py:19
  31.1 0.0 copy-done.1
  31.1 0.5 fusion.4
  31.5 2.5 %collective-permute-done.9 = bf16[4,4096]{1,0:T(4,128)(2,1)S(1)} collective-permute-done((bf16[4,4096]{1,0:T(4,128)(2,1)S(1)}, bf16[4,4096]{1,0:T(4,128)(2,1)S(1)}, u32[]{:S(2)}, u32[]{:S(2)}) %collective-permute-start.9) | collective-permute-done | bytes 32800 | tf_op jit(solution)/shard_map/ppermute | solution.py:19
  34.0 1.0 %collective-permute-start.10 = (bf16[4,4096]{1,0:T(4,128)(2,1)S(1)}, bf16[4,4096]{1,0:T(4,128)(2,1)S(1)}, u32[]{:S(2)}, u32[]{:S(2)}) collective-permute-start(bf16[4,4096]{1,0:T(4,128)(2,1)S(1)} %fusion.11), channel_id=1, source_target_pairs={{0,2},{1,3},{2,0},{3,1},{4,6},{5,7},{6,4},{7,5},{8,10},{9,11},{10,... | collective-permute-start | bytes 98312 | tf_op jit(solution)/shard_map/ppermute | solution.py:19
  35.1 2.9 %collective-permute-done.10 = bf16[4,4096]{1,0:T(4,128)(2,1)S(1)} collective-permute-done((bf16[4,4096]{1,0:T(4,128)(2,1)S(1)}, bf16[4,4096]{1,0:T(4,128)(2,1)S(1)}, u32[]{:S(2)}, u32[]{:S(2)}) %collective-permute-start.10) | collective-permute-done | bytes 32800 | tf_op jit(solution)/shard_map/ppermute | solution.py:19
  38.0 2.9 %collective-permute-start.13 = (bf16[8,4096]{1,0:T(8,128)(2,1)S(1)}, bf16[8,4096]{1,0:T(8,128)(2,1)S(1)}, u32[]{:S(2)}, u32[]{:S(2)}) collective-permute-start(bf16[8,4096]{1,0:T(8,128)(2,1)S(1)} %pad_maximum_fusion.3), channel_id=1, source_target_pairs={{0,12},{1,13},{2,14},{3,15},{4,8},{5,9},{6,10},{7,11},{8,4},{9,5},... | collective-permute-start | bytes 196616 | tf_op jit(solution)/shard_map/ppermute | solution.py:19
  41.0 0.0 collective-permute-start.12
  41.0 1.5 %collective-permute-start.11 = (bf16[8,4096]{1,0:T(8,128)(2,1)S(1)}, bf16[8,4096]{1,0:T(8,128)(2,1)S(1)}, u32[]{:S(2)}, u32[]{:S(2)}) collective-permute-start(bf16[8,4096]{1,0:T(8,128)(2,1)S(1)} %pad_maximum_fusion.3), channel_id=1, source_target_pairs={{0,8},{1,9},{2,10},{3,11},{4,12},{5,13},{6,14},{7,15},{8,0},{9,1},... | collective-permute-start | bytes 196616 | tf_op jit(solution)/shard_map/ppermute | solution.py:19
  42.5 0.7 %reshape.75 = bf16[4,2,2048]{2,1,0:T(2,128)(2,1)} reshape(bf16[4,4096]{1,0:T(4,128)(2,1)S(1)} %fusion.11) | data formatting | bytes 65536 | tf_op jit(solution)/shard_map/reshape | solution.py:107
  43.2 1.3 %collective-permute-done.13 = bf16[8,4096]{1,0:T(8,128)(2,1)S(1)} collective-permute-done((bf16[8,4096]{1,0:T(8,128)(2,1)S(1)}, bf16[8,4096]{1,0:T(8,128)(2,1)S(1)}, u32[]{:S(2)}, u32[]{:S(2)}) %collective-permute-start.13) | collective-permute-done | bytes 65568 | tf_op jit(solution)/shard_map/ppermute | solution.py:19
  44.5 0.8 %collective-permute-done.12 = bf16[8,4096]{1,0:T(8,128)(2,1)S(1)} collective-permute-done((bf16[8,4096]{1,0:T(8,128)(2,1)S(1)}, bf16[8,4096]{1,0:T(8,128)(2,1)S(1)}, u32[]{:S(2)}, u32[]{:S(2)}) %collective-permute-start.12) | collective-permute-done | bytes 65568 | tf_op jit(solution)/shard_map/ppermute | solution.py:19
  45.3 0.8 %collective-permute-done.11 = bf16[8,4096]{1,0:T(8,128)(2,1)S(1)} collective-permute-done((bf16[8,4096]{1,0:T(8,128)(2,1)S(1)}, bf16[8,4096]{1,0:T(8,128)(2,1)S(1)}, u32[]{:S(2)}, u32[]{:S(2)}) %collective-permute-start.11) | collective-permute-done | bytes 65568 | tf_op jit(solution)/shard_map/ppermute | solution.py:19
  46.1 0.1 concatenate.27
  46.2 0.1 collective-permute-start.14
  46.3 0.0 copy-start.2
  46.3 1.5 %collective-permute-done.14 = bf16[32,4096]{1,0:T(8,128)(2,1)S(1)} collective-permute-done((bf16[32,4096]{1,0:T(8,128)(2,1)S(1)}, bf16[32,4096]{1,0:T(8,128)(2,1)S(1)}, u32[]{:S(2)}, u32[]{:S(2)}) %collective-permute-start.14) | collective-permute-done | bytes 262176 | tf_op jit(solution)/shard_map/ppermute | solution.py:19
  47.8 0.1 convert_reduce_fusion.1
  47.9 1.7 %fusion.3 = bf16[256,2048]{1,0:T(8,128)(2,1)S(1)} fusion(bf16[256,64]{0,1:T(8,128)(2,1)S(1)} %fusion.12, f32[256]{0:T(256)S(1)} %get-tuple-element.39, bf16[256,4096]{1,0:T(8,128)(2,1)} %bitcast.28, bf16[64,4096]{1,0:T(8,128)(2,1)S(1)} %constant_dynamic-update-slice_fusion.5), kind=kOutput, calls=%fused_computation.10 | convolution fusion | flops 69730304 | bytes 2393088 | tf_op jit(solution)/shard_map/dot_general | solution.py:99
  49.6 0.0 copy-done.2
  49.6 0.5 fusion.2
  50.1 0.2 pad_maximum_fusion
  50.3 3.5 %copy.10 = bf16[256,2,2048]{2,1,0:T(2,128)(2,1)} copy(bf16[256,2,2048]{2,0,1:T(8,128)(2,1)S(1)} %pad_maximum_fusion) | data formatting | bytes 4194304
  53.8 1.3 %convert_reduce_fusion.3 = (f32[256]{0:T(256)}, bf16[64,256]{1,0:T(8,128)(2,1)S(1)}) fusion(f32[256]{0:T(256)S(1)} %get-tuple-element.40, bf16[64,4096]{1,0:T(8,128)(2,1)S(1)} %constant_dynamic-update-slice_fusion.5, bf16[4096,256]{0,1:T(8,128)(2,1)S(1)} %bitcast.30, f32[64,256]{1,0:T(8,128)S(1)} %get-tuple-element.43), kind=kOutput, calls=%fused_computation.33 | convolution fusion | flops 134332160 | bytes 2721792 | tf_op jit(solution)/shard_map/dot_general | solution.py:92
  55.1 0.6 %pad_maximum_fusion.4 = f32[2,2048]{1,0:T(2,128)} fusion(f32[1,2048]{1,0:T(1,128)S(1)} %bitcast.41, f32[1,2048]{1,0:T(1,128)S(1)} %bitcast.42), kind=kLoop, calls=%fused_computation.43 | loop fusion | flops 4096 | bytes 32768 | tf_op jit(solution)/shard_map/concatenate | solution.py:85
  55.8 2.1 %convolution_convert_fusion = bf16[4096,256]{1,0:T(8,128)(2,1)} fusion(bf16[4096,64]{0,1:T(8,128)(2,1)S(1)} %bitcast.31, bf16[64,256]{1,0:T(8,128)(2,1)S(1)} %get-tuple-element.45), kind=kOutput, calls=%fused_computation | convolution fusion | flops 135266304 | bytes 2654208 | tf_op jit(solution)/shard_map/dot_general | solution.py:95
  (19 shorter events, 0.3 us)
Async XLA Ops:
  0.6 17.2 %copy-start = (bf16[2,2048,256]{2,1,0:T(8,128)(2,1)S(1)}, bf16[2,2048,256]{2,1,0:T(8,128)(2,1)}, u32[]{:S(2)}) copy-start(bf16[2,2048,256]{2,1,0:T(8,128)(2,1)} %param.6) | copy-start | bytes 6291460
  1.6 5.6 %collective-permute-start = (bf16[4,4096]{1,0:T(4,128)(2,1)S(1)}, bf16[4,4096]{1,0:T(4,128)(2,1)S(1)}, u32[]{:S(2)}, u32[]{:S(2)}) collective-permute-start(bf16[4,4096]{1,0:T(4,128)(2,1)S(1)} %bitcast.36), channel_id=1, source_target_pairs={{0,2},{1,3},{2,0},{3,1},{4,6},{5,7},{6,4},{7,5},{8,10},{9,11},{10,... | collective-permute-start | bytes 98312 | tf_op jit(solution)/shard_map/ppermute | solution.py:19
  4.6 13.2 %copy-start.4 = (f32[256]{0:T(256)S(1)}, f32[256]{0:T(256)}, u32[]{:S(2)}) copy-start(f32[256]{0:T(256)} %param.7) | copy-start | bytes 3076
  7.1 23.9 %copy-start.1 = (bf16[32,8,2,2048]{3,1,2,0:T(8,128)(2,1)}, bf16[32,8,2,2048]{3,1,2,0:T(8,128)(2,1)S(1)}, u32[]{:S(2)}) copy-start(bf16[32,8,2,2048]{3,1,2,0:T(8,128)(2,1)S(1)} %copy.12) | copy-start | bytes 6291460
  7.2 6.2 %collective-permute-start.3 = (bf16[8,4096]{1,0:T(8,128)(2,1)S(1)}, bf16[8,4096]{1,0:T(8,128)(2,1)S(1)}, u32[]{:S(2)}, u32[]{:S(2)}) collective-permute-start(bf16[8,4096]{1,0:T(8,128)(2,1)S(1)} %pad_maximum_fusion.2), channel_id=1, source_target_pairs={{0,12},{1,13},{2,14},{3,15},{4,8},{5,9},{6,10},{7,11},{8,4},{9,5},... | collective-permute-start | bytes 196616 | tf_op jit(solution)/shard_map/ppermute | solution.py:19
  10.9 4.6 %collective-permute-start.2 = (bf16[8,4096]{1,0:T(8,128)(2,1)S(1)}, bf16[8,4096]{1,0:T(8,128)(2,1)S(1)}, u32[]{:S(2)}, u32[]{:S(2)}) collective-permute-start(bf16[8,4096]{1,0:T(8,128)(2,1)S(1)} %pad_maximum_fusion.2), channel_id=1, source_target_pairs={{0,4},{1,5},{2,6},{3,7},{4,0},{5,1},{6,2},{7,3},{8,12},{9,13},{10,... | collective-permute-start | bytes 196616 | tf_op jit(solution)/shard_map/ppermute | solution.py:19
  10.9 5.4 %collective-permute-start.1 = (bf16[8,4096]{1,0:T(8,128)(2,1)S(1)}, bf16[8,4096]{1,0:T(8,128)(2,1)S(1)}, u32[]{:S(2)}, u32[]{:S(2)}) collective-permute-start(bf16[8,4096]{1,0:T(8,128)(2,1)S(1)} %pad_maximum_fusion.2), channel_id=1, source_target_pairs={{0,8},{1,9},{2,10},{3,11},{4,12},{5,13},{6,14},{7,15},{8,0},{9,1},... | collective-permute-start | bytes 196616 | tf_op jit(solution)/shard_map/ppermute | solution.py:19
  16.2 1.6 %collective-permute-start.4 = (bf16[32,4096]{1,0:T(8,128)(2,1)S(1)}, bf16[32,4096]{1,0:T(8,128)(2,1)S(1)}, u32[]{:S(2)}, u32[]{:S(2)}) collective-permute-start(bf16[32,4096]{1,0:T(8,128)(2,1)S(1)} %pad_maximum_fusion.1), channel_id=1, source_target_pairs={{0,1},{1,0},{2,3},{3,2},{4,5},{5,4},{6,7},{7,6},{8,9},{9,8},{10,11... | collective-permute-start | bytes 786440 | tf_op jit(solution)/shard_map/ppermute | solution.py:19
  18.4 6.5 %copy-start.3 = (f32[2,2048]{1,0:T(2,128)S(1)}, f32[2,2048]{1,0:T(2,128)}, u32[]{:S(2)}) copy-start(f32[2,2048]{1,0:T(2,128)} %param.9) | copy-start | bytes 49156
  18.9 1.6 %collective-permute-start.5 = (bf16[32,4096]{1,0:T(8,128)(2,1)S(1)}, bf16[32,4096]{1,0:T(8,128)(2,1)S(1)}, u32[]{:S(2)}, u32[]{:S(2)}) collective-permute-start(bf16[32,4096]{1,0:T(8,128)(2,1)S(1)} %slice.86), channel_id=1, source_target_pairs={{0,1},{1,0},{2,3},{3,2},{4,5},{5,4},{6,7},{7,6},{8,9},{9,8},{10,11... | collective-permute-start | bytes 786440 | tf_op jit(solution)/shard_map/ppermute | solution.py:19
  20.6 7.5 %collective-permute-start.6 = (bf16[8,4096]{1,0:T(8,128)(2,1)S(1)}, bf16[8,4096]{1,0:T(8,128)(2,1)S(1)}, u32[]{:S(2)}, u32[]{:S(2)}) collective-permute-start(bf16[8,4096]{1,0:T(8,128)(2,1)S(1)} %get-tuple-element.36), channel_id=1, source_target_pairs={{0,8},{1,9},{2,10},{3,11},{4,12},{5,13},{6,14},{7,15},{8,0},{9,1},... | collective-permute-start | bytes 196616 | tf_op jit(solution)/shard_map/ppermute | solution.py:19
  22.7 6.5 %collective-permute-start.8 = (bf16[8,4096]{1,0:T(8,128)(2,1)S(1)}, bf16[8,4096]{1,0:T(8,128)(2,1)S(1)}, u32[]{:S(2)}, u32[]{:S(2)}) collective-permute-start(bf16[8,4096]{1,0:T(8,128)(2,1)S(1)} %get-tuple-element.37), channel_id=1, source_target_pairs={{0,12},{1,13},{2,14},{3,15},{4,8},{5,9},{6,10},{7,11},{8,4},{9,5},... | collective-permute-start | bytes 196616 | tf_op jit(solution)/shard_map/ppermute | solution.py:19
  24.9 5.1 %collective-permute-start.7 = (bf16[8,4096]{1,0:T(8,128)(2,1)S(1)}, bf16[8,4096]{1,0:T(8,128)(2,1)S(1)}, u32[]{:S(2)}, u32[]{:S(2)}) collective-permute-start(bf16[8,4096]{1,0:T(8,128)(2,1)S(1)} %get-tuple-element.38), channel_id=1, source_target_pairs={{0,4},{1,5},{2,6},{3,7},{4,0},{5,1},{6,2},{7,3},{8,12},{9,13},{10,... | collective-permute-start | bytes 196616 | tf_op jit(solution)/shard_map/ppermute | solution.py:19
  30.0 4.0 %collective-permute-start.9 = (bf16[4,4096]{1,0:T(4,128)(2,1)S(1)}, bf16[4,4096]{1,0:T(4,128)(2,1)S(1)}, u32[]{:S(2)}, u32[]{:S(2)}) collective-permute-start(bf16[4,4096]{1,0:T(4,128)(2,1)S(1)} %slice.87), channel_id=1, source_target_pairs={{0,2},{1,3},{2,0},{3,1},{4,6},{5,7},{6,4},{7,5},{8,10},{9,11},{10,... | collective-permute-start | bytes 98312 | tf_op jit(solution)/shard_map/ppermute | solution.py:19
  34.0 4.0 %collective-permute-start.10 = (bf16[4,4096]{1,0:T(4,128)(2,1)S(1)}, bf16[4,4096]{1,0:T(4,128)(2,1)S(1)}, u32[]{:S(2)}, u32[]{:S(2)}) collective-permute-start(bf16[4,4096]{1,0:T(4,128)(2,1)S(1)} %fusion.11), channel_id=1, source_target_pairs={{0,2},{1,3},{2,0},{3,1},{4,6},{5,7},{6,4},{7,5},{8,10},{9,11},{10,... | collective-permute-start | bytes 98312 | tf_op jit(solution)/shard_map/ppermute | solution.py:19
  38.0 6.5 %collective-permute-start.13 = (bf16[8,4096]{1,0:T(8,128)(2,1)S(1)}, bf16[8,4096]{1,0:T(8,128)(2,1)S(1)}, u32[]{:S(2)}, u32[]{:S(2)}) collective-permute-start(bf16[8,4096]{1,0:T(8,128)(2,1)S(1)} %pad_maximum_fusion.3), channel_id=1, source_target_pairs={{0,12},{1,13},{2,14},{3,15},{4,8},{5,9},{6,10},{7,11},{8,4},{9,5},... | collective-permute-start | bytes 196616 | tf_op jit(solution)/shard_map/ppermute | solution.py:19
  41.0 4.3 %collective-permute-start.12 = (bf16[8,4096]{1,0:T(8,128)(2,1)S(1)}, bf16[8,4096]{1,0:T(8,128)(2,1)S(1)}, u32[]{:S(2)}, u32[]{:S(2)}) collective-permute-start(bf16[8,4096]{1,0:T(8,128)(2,1)S(1)} %pad_maximum_fusion.3), channel_id=1, source_target_pairs={{0,4},{1,5},{2,6},{3,7},{4,0},{5,1},{6,2},{7,3},{8,12},{9,13},{10,... | collective-permute-start | bytes 196616 | tf_op jit(solution)/shard_map/ppermute | solution.py:19
  41.0 5.2 %collective-permute-start.11 = (bf16[8,4096]{1,0:T(8,128)(2,1)S(1)}, bf16[8,4096]{1,0:T(8,128)(2,1)S(1)}, u32[]{:S(2)}, u32[]{:S(2)}) collective-permute-start(bf16[8,4096]{1,0:T(8,128)(2,1)S(1)} %pad_maximum_fusion.3), channel_id=1, source_target_pairs={{0,8},{1,9},{2,10},{3,11},{4,12},{5,13},{6,14},{7,15},{8,0},{9,1},... | collective-permute-start | bytes 196616 | tf_op jit(solution)/shard_map/ppermute | solution.py:19
  46.2 1.6 %collective-permute-start.14 = (bf16[32,4096]{1,0:T(8,128)(2,1)S(1)}, bf16[32,4096]{1,0:T(8,128)(2,1)S(1)}, u32[]{:S(2)}, u32[]{:S(2)}) collective-permute-start(bf16[32,4096]{1,0:T(8,128)(2,1)S(1)} %concatenate.27), channel_id=1, source_target_pairs={{0,1},{1,0},{2,3},{3,2},{4,5},{5,4},{6,7},{7,6},{8,9},{9,8},{10,11... | collective-permute-start | bytes 786440 | tf_op jit(solution)/shard_map/ppermute | solution.py:19
  46.3 3.3 %copy-start.2 = (bf16[32,8,2,2048]{3,1,2,0:T(8,128)(2,1)S(1)}, bf16[32,8,2,2048]{3,1,2,0:T(8,128)(2,1)}, u32[]{:S(2)}) copy-start(bf16[32,8,2,2048]{3,1,2,0:T(8,128)(2,1)} %copy-done.1) | copy-start | bytes 6291460
